TPU v7x, 32 devices: a whole 2x2x4 slice. The times are simulated.
32 devices in a mesh: ka: 16 (over z, x, core), sp: 2 (over y).
Axes of the slice: x: 2, y: 2, z: 4, core: 2. Of those that a mesh axis runs over, the one named last changes fastest.
Arguments:
- bloch_index: int32 [16, 2], P('ka'), may hold values from 0 to 63
- material: int32 [32, 64, 128], P('sp'), may hold values from 0 to 2
- permittivity: float32 [3], replicated, may hold values from 1 to 12
- absorption_peak: float32 [1], replicated, may hold values from 0.25 to 2
- source_sheet: float32 [16, 2, 32, 64], P('ka', None, 'sp'), may hold values from -6 to 6
- waveform: float32 [10], replicated, may hold values from -6 to 6
- electric_in: bfloat16 [16, 6, 32, 64, 128], P('ka', None, 'sp'), may hold values from -12 to 12
- magnetic_in: bfloat16 [16, 6, 32, 64, 128], P('ka', None, 'sp'), may hold values from -12 to 12
Outputs:
- electric_out: float32 [16, 6, 32, 64, 128], P('ka', None, 'sp')
- magnetic_out: float32 [16, 6, 32, 64, 128], P('ka', None, 'sp')
- reflected: float32 [16, 2], P('ka')
- reflected_mean: float32 [2], replicated
All inputs are finite; a program needn't handle non-finite values.
Results may differ from a plain program's by a relative error of at most 0.0003.
Values sent between devices are 32-bit elements; how exact they have to be, the bound alone decides.
A program may use at most 64 MiB of HBM per device.

v0:
```python
import jax
import jax.numpy as jnp
from jax import lax
from jax.experimental import pallas as pl
from jax.experimental.pallas import tpu as pltpu
from jax.sharding import PartitionSpec as P

PML = 16
INTERVAL = 5
MPHASE = 64
NMAT = 3
TIME_STEP = 0.5
MESH = pl.DeviceIdType.MESH


def rotate(couple, cosine, sine):
    return (couple[0] * cosine - couple[1] * sine, couple[0] * sine + couple[1] * cosine)


def minus(left, right):
    return (left[0] - right[0], left[1] - right[1])


def plus(left, right):
    return (left[0] + right[0], left[1] + right[1])


def relax(couple, change, keep, gain):
    return tuple(keep * c + gain * d for c, d in zip(couple, change))


def kernel(
    bloch_in,
    perm_in,
    peak_in,
    wave_in,
    material_in,
    sheet_in,
    e_hbm,
    h_hbm,
    e_ref,
    h_ref,
    reflected_ref,
    mean_ref,
    bloch_ref,
    perm_ref,
    peak_ref,
    wave_ref,
    material_ref,
    sheet_ref,
    e_in,
    h_in,
    report_ref,
    got_report,
    keep_ref,
    gain_ref,
    drive_ref,
    out_e,
    out_w,
    got_e,
    got_w,
    send_e,
    send_w,
    recv_e,
    recv_w,
    load_sem,
    send_report,
    recv_report,
):
    rows, width, depth = material_ref.shape
    steps = wave_ref.shape[0]
    slabs = lax.axis_size("sp")
    slab = lax.axis_index("sp")
    upper = lax.rem(slab + 1, slabs)
    lower = lax.rem(slab + slabs - 1, slabs)

    groups = lax.axis_size("ka")
    group = lax.axis_index("ka")
    everyone = groups * slabs
    me = group * slabs + slab

    def place(at):
        return {"ka": lax.div(at, slabs), "sp": lax.rem(at, slabs)}

    last_row = rows - 1
    loads = [
        pltpu.make_async_copy(src, dst, load_sem.at[at])
        for at, (src, dst) in enumerate(
            (
                (e_hbm.at[0, :, last_row], e_in.at[0, :, last_row]),
                (h_hbm.at[0, :, last_row], h_in.at[0, :, last_row]),
                (e_hbm.at[0, :, 0], e_in.at[0, :, 0]),
                (h_hbm.at[0, :, 0], h_in.at[0, :, 0]),
                (bloch_in, bloch_ref),
                (perm_in, perm_ref),
                (peak_in, peak_ref),
                (wave_in, wave_ref),
                (e_hbm.at[0, :, 1:last_row], e_in.at[0, :, 1:last_row]),
                (h_hbm.at[0, :, 1:last_row], h_in.at[0, :, 1:last_row]),
                (material_in, material_ref),
                (sheet_in, sheet_ref),
            )
        )
    ]
    for load in loads:
        load.start()

    barrier = pltpu.get_barrier_semaphore()

    def greet(offset, carry):
        other = lax.rem(me + offset, everyone)
        pl.semaphore_signal(barrier, inc=1, device_id=place(other), device_id_type=MESH)
        return carry

    lax.fori_loop(1, everyone, greet, 0)
    for load in loads[4:8]:
        load.wait()

    height = lax.broadcasted_iota(jnp.int32, (8, depth), 1).astype(jnp.float32)
    low_depth = jnp.maximum(PML - height, 0.0) / PML
    high_depth = jnp.maximum(height - (depth - 1 - PML), 0.0) / PML
    conduct = peak_ref[0] * (
        low_depth * low_depth * low_depth + high_depth * high_depth * high_depth
    )
    half_mag = conduct * (0.5 * TIME_STEP)
    h_keep = ((1.0 - half_mag) / (1.0 + half_mag))[0:1]
    h_gain = (-TIME_STEP / (1.0 + half_mag))[0:1]
    tables = []
    for level in range(NMAT):
        relative = jnp.full((8, depth), perm_ref[level], jnp.float32)
        half_ele = conduct * (0.5 * TIME_STEP) / relative
        tables.append(
            (
                ((1.0 - half_ele) / (1.0 + half_ele))[0:1],
                (TIME_STEP / relative / (1.0 + half_ele))[0:1],
            )
        )

    def trig(member):
        angle = jnp.full((8, depth), bloch_ref[0, member], jnp.int32).astype(jnp.float32)
        angle = 2.0 * jnp.pi * angle / MPHASE
        return jnp.cos(angle)[0:1], jnp.sin(angle)[0:1]

    cos_x, sin_x = trig(0)
    cos_y, sin_y = trig(1)
    at_end = (slab == slabs - 1).astype(jnp.float32)
    at_start = (slab == 0).astype(jnp.float32)
    end_cos = at_end * cos_x + (1.0 - at_end)
    end_sin = at_end * sin_x
    start_cos = at_start * cos_x + (1.0 - at_start)
    start_sin = -at_start * sin_x

    lane = lax.broadcasted_iota(jnp.int32, (width, depth), 1)
    last_lane = lane == depth - 1
    first_lane = lane == 0
    sub = lax.broadcasted_iota(jnp.int32, (8, depth), 0)

    def above_z(couple):
        return tuple(jnp.where(last_lane, 0.0, pltpu.roll(v, depth - 1, 1)) for v in couple)

    def below_z(couple):
        return tuple(jnp.where(first_lane, 0.0, pltpu.roll(v, 1, 1)) for v in couple)

    def above_y(couple):
        moved = tuple(pltpu.roll(v, width - 1, 0) for v in couple)
        tail = tuple(v[width - 8 :] for v in moved)
        turned = rotate(tail, cos_y, sin_y)
        return tuple(
            jnp.concatenate([v[: width - 8], jnp.where(sub == 7, r, w)], axis=0)
            for v, r, w in zip(moved, turned, tail)
        )

    def below_y(couple):
        moved = tuple(pltpu.roll(v, 1, 0) for v in couple)
        head = tuple(v[:8] for v in moved)
        turned = rotate(head, cos_y, -sin_y)
        return tuple(
            jnp.concatenate([jnp.where(sub == 0, r, w), v[8:]], axis=0)
            for v, r, w in zip(moved, turned, head)
        )

    def get(ref, member, x):
        return (ref[0, 2 * member, x], ref[0, 2 * member + 1, x])

    def put(ref, member, x, couple):
        ref[0, 2 * member, x] = couple[0]
        ref[0, 2 * member + 1, x] = couple[1]

    def get_plane(ref, slot, member):
        return (ref[slot, 2 * member], ref[slot, 2 * member + 1])

    def put_plane(ref, slot, member, couple):
        ref[slot, 2 * member] = couple[0]
        ref[slot, 2 * member + 1] = couple[1]

    def hx_plane(x):
        ey, ez = get(e_ref, 1, x), get(e_ref, 2, x)
        change = minus(minus(above_y(ez), ez), minus(above_z(ey), ey))
        put(h_ref, 0, x, relax(get(h_ref, 0, x), change, h_keep, h_gain))

    def h_plane(x, carry):
        hx_plane(x)
        ex, ey, ez = get(e_ref, 0, x), get(e_ref, 1, x), get(e_ref, 2, x)
        dx_ez = minus(get(e_ref, 2, x + 1), ez)
        dx_ey = minus(get(e_ref, 1, x + 1), ey)
        change = minus(minus(above_z(ex), ex), dx_ez)
        put(h_ref, 1, x, relax(get(h_ref, 1, x), change, h_keep, h_gain))
        change = minus(dx_ey, minus(above_y(ex), ex))
        put(h_ref, 2, x, relax(get(h_ref, 2, x), change, h_keep, h_gain))
        return carry

    def partial_h(slot):
        x = rows - 1
        ex, ey, ez = get(e_ref, 0, x), get(e_ref, 1, x), get(e_ref, 2, x)
        change = plus(minus(above_z(ex), ex), ez)
        put_plane(out_w, slot, 0, relax(get(h_ref, 1, x), change, h_keep, h_gain))
        change = minus(minus(ex, above_y(ex)), ey)
        put_plane(out_w, slot, 1, relax(get(h_ref, 2, x), change, h_keep, h_gain))

    def complete_h(slot):
        x = rows - 1
        beyond_y = rotate(get_plane(got_e, slot, 0), end_cos, end_sin)
        beyond_z = rotate(get_plane(got_e, slot, 1), end_cos, end_sin)
        w_y, w_z = get_plane(out_w, slot, 0), get_plane(out_w, slot, 1)
        put(h_ref, 1, x, tuple(w - h_gain * b for w, b in zip(w_y, beyond_z)))
        put(h_ref, 2, x, tuple(w + h_gain * b for w, b in zip(w_z, beyond_y)))

    def e_update(x, drive, hy_prev, hz_prev):
        hx, hy, hz = get(h_ref, 0, x), get(h_ref, 1, x), get(h_ref, 2, x)
        keep, gain = keep_ref[x], gain_ref[x]
        change = minus(minus(hz, below_y(hz)), minus(hy, below_z(hy)))
        change = (change[0] - drive * drive_ref[0, x], change[1] - drive * drive_ref[1, x])
        put(e_ref, 0, x, relax(get(e_ref, 0, x), change, keep, gain))
        change = minus(minus(hx, below_z(hx)), minus(hz, hz_prev))
        ey = relax(get(e_ref, 1, x), change, keep, gain)
        put(e_ref, 1, x, ey)
        change = minus(minus(hy, hy_prev), minus(hx, below_y(hx)))
        ez = relax(get(e_ref, 2, x), change, keep, gain)
        put(e_ref, 2, x, ez)
        return ey, ez

    def e_first(slot, drive):
        ey, ez = get(e_ref, 1, 0), get(e_ref, 2, 0)
        turned_y = rotate(get_plane(got_w, slot, 0), start_cos, start_sin)
        turned_z = rotate(get_plane(got_w, slot, 1), start_cos, start_sin)
        hy_prev = tuple(w - h_gain * e for w, e in zip(turned_y, ez))
        hz_prev = tuple(w + h_gain * e for w, e in zip(turned_z, ey))
        return e_update(0, drive, hy_prev, hz_prev)

    def copy_e(slot):
        return pltpu.make_async_remote_copy(
            src_ref=out_e.at[slot],
            dst_ref=got_e.at[slot],
            send_sem=send_e.at[slot],
            recv_sem=recv_e.at[slot],
            device_id={"sp": lower},
            device_id_type=MESH,
        )

    def copy_w(slot):
        return pltpu.make_async_remote_copy(
            src_ref=out_w.at[slot],
            dst_ref=got_w.at[slot],
            send_sem=send_w.at[slot],
            recv_sem=recv_w.at[slot],
            device_id={"sp": upper},
            device_id_type=MESH,
        )

    def widen(x, carry):
        for member in range(6):
            e_ref[0, member, x] = e_in[0, member, x].astype(jnp.float32)
            h_ref[0, member, x] = h_in[0, member, x].astype(jnp.float32)
        return carry

    for load in loads[0:4]:
        load.wait()
    widen(rows - 1, 0)
    partial_h(0)
    widen(0, 0)
    for member in range(2):
        put_plane(out_e, 0, member, get(e_ref, 1 + member, 0))
    pl.semaphore_wait(barrier, everyone - 1)
    copy_w(0).start()
    copy_e(0).start()
    for load in loads[8:]:
        load.wait()
    lax.fori_loop(1, rows - 1, widen, 0)

    report_ref[...] = jnp.zeros_like(report_ref)
    square = lax.broadcasted_iota(jnp.int32, (width, width), 0) == lax.broadcasted_iota(
        jnp.int32, (width, width), 1
    )

    def prepare(x, carry):
        kind = material_ref[x]
        keep, gain = tables[0]
        for level in range(1, NMAT):
            keep = jnp.where(kind == level, tables[level][0], keep)
            gain = jnp.where(kind == level, tables[level][1], gain)
        keep_ref[x] = keep
        gain_ref[x] = gain
        for part in range(2):
            row = sheet_ref[0, part, pl.ds(x, 1), :]
            column = jnp.sum(jnp.where(square, row, 0.0), axis=1, keepdims=True)
            drive_ref[part, x] = jnp.where(lane == PML + 2, column, 0.0)
        return carry

    lax.fori_loop(0, rows, prepare, 0)

    def power(x, total):
        for member in range(4):
            value = e_ref[0, member, x]
            total = total + value * value
        return total

    def step(t, carry):
        slot = lax.rem(t, 2)
        later = lax.rem(t + 1, 2)
        drive = wave_ref[t]
        even = slot == 0
        ready = jnp.logical_and(t >= 1, t < steps - 1)
        snapshot = lax.rem(t + 1, INTERVAL) == 0
        empty = jnp.zeros((width, depth), jnp.float32)

        def left():
            copy_w(slot).wait_recv()
            ey, ez = e_first(slot, drive)

            @pl.when(ready)
            def _():
                copy_e(later).wait_send()

            @pl.when(t < steps - 1)
            def _():
                put_plane(out_e, later, 0, ey)
                put_plane(out_e, later, 1, ez)
                copy_e(later).start()

        def right():
            copy_e(slot).wait_recv()
            complete_h(slot)
            e_update(rows - 1, drive, get(h_ref, 1, rows - 2), get(h_ref, 2, rows - 2))

            @pl.when(ready)
            def _():
                copy_w(later).wait_send()

            @pl.when(t < steps - 1)
            def _():
                partial_h(later)
                copy_w(later).start()

        def inner(x, held):
            e_update(x, drive, get(h_ref, 1, x - 1), get(h_ref, 2, x - 1))
            return held

        lax.fori_loop(0, rows - 1, h_plane, 0)
        hx_plane(rows - 1)
        pl.when(even)(left)
        pl.when(jnp.logical_not(even))(right)
        lax.fori_loop(1, rows - 1, inner, 0)

        @pl.when(snapshot)
        def _():
            total = lax.fori_loop(1, rows - 1, power, empty)
            report_ref[pl.ds(lax.div(t, INTERVAL), 1)] = jnp.sum(total, axis=0, keepdims=True)

        pl.when(even)(right)
        pl.when(jnp.logical_not(even))(left)

        @pl.when(snapshot)
        def _():
            total = power(0, power(rows - 1, empty))
            at = lax.div(t, INTERVAL)
            report_ref[pl.ds(at, 1)] += jnp.sum(total, axis=0, keepdims=True)

        return carry

    lax.fori_loop(0, steps, step, 0)

    def tell(offset):
        return pltpu.make_async_remote_copy(
            src_ref=report_ref,
            dst_ref=got_report.at[me],
            send_sem=send_report,
            recv_sem=recv_report,
            device_id=place(lax.rem(me + offset, everyone)),
            device_id_type=MESH,
        )

    def tell_start(offset, carry):
        tell(offset).start()
        return carry

    lax.fori_loop(1, everyone, tell_start, 0)
    got_report[me] = report_ref[...]
    for t in (steps - 2, steps - 1):
        copy_e(t % 2).wait_send()
        copy_w(t % 2).wait_send()
    everything = got_report.at[pl.ds(0, everyone - 1)]
    pltpu.make_async_copy(everything, everything, recv_report).wait()
    pltpu.make_async_copy(everything, everything, send_report).wait()

    def gather(at, held):
        value = got_report[at]
        ours = (lax.div(at, slabs) == group).astype(jnp.float32)
        return held[0] + value, held[1] + ours * value

    zero = jnp.zeros(report_ref.shape, jnp.float32)
    total, ours = lax.fori_loop(0, everyone, gather, (zero, zero))
    cells = rows * slabs * width
    reflected_ref[...] = ours / cells
    mean_ref[...] = total / cells / groups


def one_point(bloch, material, permittivity, peak, sheet, waveform, electric, magnetic):
    rows, width, depth = material.shape
    snaps = waveform.shape[0] // INTERVAL
    everyone = lax.axis_size("ka") * lax.axis_size("sp")
    hbm = pl.BlockSpec(memory_space=pltpu.HBM)
    lines = -(-snaps // 8) * 8
    vmem = pl.BlockSpec(memory_space=pltpu.VMEM)
    plane = (2, 4, width, depth)
    f32 = jnp.float32
    return pl.pallas_call(
        kernel,
        out_shape=(
            jax.ShapeDtypeStruct(electric.shape, f32),
            jax.ShapeDtypeStruct(magnetic.shape, f32),
            jax.ShapeDtypeStruct((lines, depth), f32),
            jax.ShapeDtypeStruct((lines, depth), f32),
        ),
        in_specs=[hbm] * 8,
        out_specs=(vmem, vmem, vmem, vmem),
        scratch_shapes=[
            pltpu.SMEM(bloch.shape, jnp.int32),
            pltpu.SMEM(permittivity.shape, f32),
            pltpu.SMEM(peak.shape, f32),
            pltpu.SMEM(waveform.shape, f32),
            pltpu.VMEM(material.shape, jnp.int32),
            pltpu.VMEM(sheet.shape, f32),
            pltpu.VMEM(electric.shape, electric.dtype),
            pltpu.VMEM(magnetic.shape, magnetic.dtype),
            pltpu.VMEM((lines, depth), f32),
            pltpu.VMEM((everyone, lines, depth), f32),
            pltpu.VMEM((rows, width, depth), f32),
            pltpu.VMEM((rows, width, depth), f32),
            pltpu.VMEM((2, rows, width, depth), f32),
            pltpu.VMEM(plane, f32),
            pltpu.VMEM(plane, f32),
            pltpu.VMEM(plane, f32),
            pltpu.VMEM(plane, f32),
            pltpu.SemaphoreType.DMA((2,)),
            pltpu.SemaphoreType.DMA((2,)),
            pltpu.SemaphoreType.DMA((2,)),
            pltpu.SemaphoreType.DMA((2,)),
            pltpu.SemaphoreType.DMA((12,)),
            pltpu.SemaphoreType.DMA,
            pltpu.SemaphoreType.DMA,
        ],
        compiler_params=pltpu.CompilerParams(
            collective_id=0, has_side_effects=True, vmem_limit_bytes=40 * 1024 * 1024
        ),
    )(*((v if v.shape == (1,) else pltpu.with_memory_space_constraint(v, pltpu.HBM)) for v in (bloch, permittivity, peak, waveform, material, sheet, electric, magnetic)))


def on_device(
    bloch_index,
    material,
    permittivity,
    absorption_peak,
    source_sheet,
    waveform,
    electric_in,
    magnetic_in,
):
    points = bloch_index.shape[0]
    results = [
        one_point(
            bloch_index[p : p + 1],
            material,
            permittivity,
            absorption_peak,
            source_sheet[p : p + 1],
            waveform,
            electric_in[p : p + 1],
            magnetic_in[p : p + 1],
        )
        for p in range(points)
    ]
    electric_out = jnp.concatenate([r[0] for r in results], 0)
    magnetic_out = jnp.concatenate([r[1] for r in results], 0)
    snaps = waveform.shape[0] // INTERVAL
    reflected = jnp.stack([r[2][:snaps, PML + 6] for r in results], 0)
    reflected_mean = sum(r[3][:snaps, PML + 6] for r in results) / points
    return (electric_out, magnetic_out, reflected, reflected_mean)


def solution(mesh):
    in_specs = (
        P("ka", None),
        P("sp", None, None),
        P(),
        P(),
        P("ka", None, "sp", None),
        P(),
        P("ka", None, "sp", None, None),
        P("ka", None, "sp", None, None),
    )
    out_specs = (
        P("ka", None, "sp", None, None),
        P("ka", None, "sp", None, None),
        P("ka", None),
        P(),
    )
    return jax.shard_map(
        on_device, mesh=mesh, in_specs=in_specs, out_specs=out_specs, check_vma=False
    )
```

profile of v0, /device:TPU:0, one launch (start us, length us, event | category | flops | bytes accessed | tf_op | source)
XLA Modules:
  0.0 74.9 jit_solution(548877737845055565)
XLA Ops:
  1.3 69.6 %shard_map.111 = (f32[1,6,16,64,128]{4,3,2,1,0:T(8,128)S(1)}, f32[1,6,16,64,128]{4,3,2,1,0:T(8,128)S(1)}, f32[8,128]{1,0:T(8,128)S(1)}, f32[8,128]{1,0:T(8,128)S(1)}) custom-call(s32[1,2]{1,0:T(1,128)} %bloch_in.1, f32[3]{0:T(128)} %perm_in.1, f32[1]{0:T(128)S(6)} %copy.14.peak_in, f32[10]{0:T(128)} %wave_in.1, s32[16,64,128]{2,1,0:T(8,128)} %material_in.1, ...), custom_call_target="tpu_custom_call" | custom-call | tf_op jit(solution)/shard_map/pallas_call | solution.py:426
  70.9 0.7 slice_reduce_fusion
  71.6 1.7 %copy.15 = f32[1,6,16,64,128]{4,3,2,1,0:T(8,128)} copy(f32[1,6,16,64,128]{4,3,2,1,0:T(8,128)S(1)} %get-tuple-element.18) | data formatting | bytes 6291456
  73.3 1.7 %copy.16 = f32[1,6,16,64,128]{4,3,2,1,0:T(8,128)} copy(f32[1,6,16,64,128]{4,3,2,1,0:T(8,128)S(1)} %get-tuple-element.19) | data formatting | bytes 6291456
where the time goes:
time: 75.1 us; the launch traced here: 74.9 us
  Pallas kernels  69.6 us (93%)
  local copies, waits for them, and re-layouts  4.06 us (5%)
  between operations  1.29 us (2%)
    pallas_call x1, Pallas kernels, one_point(): pl.pallas_call(kernel, out_shape=(jax.ShapeDtypeStruct(electric.shape, f3...  69.6 us
    unnamed x2, local copies, waits for them, and re-layouts  3.33 us

commit v1 on v0

--- a/solution.py
+++ b/solution.py
@@ -40,8 +40,7 @@
     h_hbm,
     e_ref,
     h_ref,
-    reflected_ref,
-    mean_ref,
+    power_ref,
     bloch_ref,
     perm_ref,
     peak_ref,
@@ -59,13 +58,20 @@
     out_w,
     got_e,
     got_w,
+    tiny_e,
+    tiny_w,
+    got_tiny_e,
+    got_tiny_w,
     send_e,
     send_w,
     recv_e,
     recv_w,
+    send_tiny,
+    recv_tiny,
     load_sem,
     send_report,
     recv_report,
+    entered,
 ):
     rows, width, depth = material_ref.shape
     steps = wave_ref.shape[0]
@@ -87,9 +93,9 @@
         pltpu.make_async_copy(src, dst, load_sem.at[at])
         for at, (src, dst) in enumerate(
             (
+                (e_hbm.at[0, :, 0], e_in.at[0, :, 0]),
                 (e_hbm.at[0, :, last_row], e_in.at[0, :, last_row]),
                 (h_hbm.at[0, :, last_row], h_in.at[0, :, last_row]),
-                (e_hbm.at[0, :, 0], e_in.at[0, :, 0]),
                 (h_hbm.at[0, :, 0], h_in.at[0, :, 0]),
                 (bloch_in, bloch_ref),
                 (perm_in, perm_ref),
@@ -107,12 +113,38 @@
 
     barrier = pltpu.get_barrier_semaphore()
 
-    def greet(offset, carry):
-        other = lax.rem(me + offset, everyone)
+    def greet(other):
         pl.semaphore_signal(barrier, inc=1, device_id=place(other), device_id_type=MESH)
-        return carry
-
-    lax.fori_loop(1, everyone, greet, 0)
+
+    bits = everyone.bit_length() - 1
+    hypercube = everyone == 1 << bits
+    rounds = bits - 1 if hypercube else 0
+    greeted = bits + 2 if hypercube else everyone - 1
+
+    def partner(bit):
+        return me + (1 << bit) * (1 - 2 * lax.rem(lax.div(me, 1 << bit), 2))
+
+    if hypercube:
+        greet(group * slabs + lower)
+        greet(group * slabs + upper)
+        for bit in range(bits):
+            greet(partner(bit))
+    else:
+
+        def greet_at(offset, carry):
+            greet(lax.rem(me + offset, everyone))
+            return carry
+
+        lax.fori_loop(1, everyone, greet_at, 0)
+
+    def spread(turn):
+        pl.semaphore_signal(
+            entered.at[turn], inc=1, device_id=place(partner(turn)), device_id_type=MESH
+        )
+
+    def learn(turn):
+        pl.semaphore_wait(entered.at[turn], 1)
+
     for load in loads[4:8]:
         load.wait()
 
@@ -225,17 +257,25 @@
         put(h_ref, 1, x, tuple(w - h_gain * b for w, b in zip(w_y, beyond_z)))
         put(h_ref, 2, x, tuple(w + h_gain * b for w, b in zip(w_z, beyond_y)))
 
+    def new_ex(x, drive, hy, hz):
+        change = minus(minus(hz, below_y(hz)), minus(hy, below_z(hy)))
+        change = (change[0] - drive * drive_ref[0, x], change[1] - drive * drive_ref[1, x])
+        return relax(get(e_ref, 0, x), change, keep_ref[x], gain_ref[x])
+
+    def new_ey(x, hx, hz, hz_prev):
+        change = minus(minus(hx, below_z(hx)), minus(hz, hz_prev))
+        return relax(get(e_ref, 1, x), change, keep_ref[x], gain_ref[x])
+
+    def new_ez(x, hx, hy, hy_prev):
+        change = minus(minus(hy, hy_prev), minus(hx, below_y(hx)))
+        return relax(get(e_ref, 2, x), change, keep_ref[x], gain_ref[x])
+
     def e_update(x, drive, hy_prev, hz_prev):
         hx, hy, hz = get(h_ref, 0, x), get(h_ref, 1, x), get(h_ref, 2, x)
-        keep, gain = keep_ref[x], gain_ref[x]
-        change = minus(minus(hz, below_y(hz)), minus(hy, below_z(hy)))
-        change = (change[0] - drive * drive_ref[0, x], change[1] - drive * drive_ref[1, x])
-        put(e_ref, 0, x, relax(get(e_ref, 0, x), change, keep, gain))
-        change = minus(minus(hx, below_z(hx)), minus(hz, hz_prev))
-        ey = relax(get(e_ref, 1, x), change, keep, gain)
+        put(e_ref, 0, x, new_ex(x, drive, hy, hz))
+        ey = new_ey(x, hx, hz, hz_prev)
         put(e_ref, 1, x, ey)
-        change = minus(minus(hy, hy_prev), minus(hx, below_y(hx)))
-        ez = relax(get(e_ref, 2, x), change, keep, gain)
+        ez = new_ez(x, hx, hy, hy_prev)
         put(e_ref, 2, x, ez)
         return ey, ez
 
@@ -267,30 +307,57 @@
             device_id_type=MESH,
         )
 
+    square = lax.broadcasted_iota(jnp.int32, (width, width), 0) == lax.broadcasted_iota(
+        jnp.int32, (width, width), 1
+    )
+    monitor = PML + 6
+
+    def row_of(value, z):
+        column = jnp.sum(jnp.where(lane == z, value, 0.0), axis=1, keepdims=True)
+        return jnp.sum(jnp.where(square, column, 0.0), axis=0, keepdims=True)
+
+    def at_lane(row, z):
+        column = jnp.sum(jnp.where(square, row, 0.0), axis=1, keepdims=True)
+        return jnp.where(lane == z, column, 0.0)
+
+    def copy_tiny(src, dst, at, other):
+        return pltpu.make_async_remote_copy(
+            src_ref=src,
+            dst_ref=dst,
+            send_sem=send_tiny.at[at],
+            recv_sem=recv_tiny.at[at],
+            device_id={"sp": other},
+            device_id_type=MESH,
+        )
+
+    def copy_tiny_e():
+        return copy_tiny(tiny_e, got_tiny_e, 0, lower)
+
+    def copy_tiny_w():
+        return copy_tiny(tiny_w, got_tiny_w, 1, upper)
+
     def widen(x, carry):
         for member in range(6):
             e_ref[0, member, x] = e_in[0, member, x].astype(jnp.float32)
             h_ref[0, member, x] = h_in[0, member, x].astype(jnp.float32)
         return carry
 
-    for load in loads[0:4]:
+    loads[0].wait()
+    for member in range(4):
+        out_e[0, member] = e_in[0, 2 + member, 0].astype(jnp.float32)
+    pl.semaphore_wait(barrier, greeted)
+    copy_e(0).start()
+    for load in loads[1:4]:
         load.wait()
     widen(rows - 1, 0)
     partial_h(0)
+    copy_w(0).start()
     widen(0, 0)
-    for member in range(2):
-        put_plane(out_e, 0, member, get(e_ref, 1 + member, 0))
-    pl.semaphore_wait(barrier, everyone - 1)
-    copy_w(0).start()
-    copy_e(0).start()
     for load in loads[8:]:
         load.wait()
     lax.fori_loop(1, rows - 1, widen, 0)
 
     report_ref[...] = jnp.zeros_like(report_ref)
-    square = lax.broadcasted_iota(jnp.int32, (width, width), 0) == lax.broadcasted_iota(
-        jnp.int32, (width, width), 1
-    )
 
     def prepare(x, carry):
         kind = material_ref[x]
@@ -314,70 +381,100 @@
             total = total + value * value
         return total
 
+    row_lane = lax.broadcasted_iota(jnp.int32, (1, depth), 1)
+    empty = jnp.zeros((width, depth), jnp.float32)
+    last_snapshot = steps % INTERVAL == 0
+
+    def note(total, at):
+        amount = jnp.sum(jnp.where(lane == monitor, total, 0.0), axis=0, keepdims=True)
+        amount = jnp.sum(amount, axis=1, keepdims=True)
+        report_ref[...] += jnp.where(row_lane == at, amount, 0.0)
+
     def step(t, carry):
         slot = lax.rem(t, 2)
         later = lax.rem(t + 1, 2)
         drive = wave_ref[t]
         even = slot == 0
-        ready = jnp.logical_and(t >= 1, t < steps - 1)
         snapshot = lax.rem(t + 1, INTERVAL) == 0
-        empty = jnp.zeros((width, depth), jnp.float32)
+        before_last = t == steps - 2
 
         def left():
             copy_w(slot).wait_recv()
             ey, ez = e_first(slot, drive)
 
-            @pl.when(ready)
+            @pl.when(t >= 1)
             def _():
                 copy_e(later).wait_send()
 
-            @pl.when(t < steps - 1)
-            def _():
-                put_plane(out_e, later, 0, ey)
-                put_plane(out_e, later, 1, ez)
-                copy_e(later).start()
+            put_plane(out_e, later, 0, ey)
+            put_plane(out_e, later, 1, ez)
+
+            if last_snapshot:
+
+                @pl.when(before_last)
+                def _():
+                    for part in range(2):
+                        tiny_e[part : part + 1] = row_of(ey[part], monitor)
+                        tiny_e[2 + part : 3 + part] = row_of(ez[part], monitor)
+                        tiny_e[4 + part : 5 + part] = row_of(ez[part], monitor - 1)
+                    copy_tiny_e().start()
+
+            copy_e(later).start()
 
         def right():
             copy_e(slot).wait_recv()
             complete_h(slot)
             e_update(rows - 1, drive, get(h_ref, 1, rows - 2), get(h_ref, 2, rows - 2))
 
-            @pl.when(ready)
+            @pl.when(t >= 1)
             def _():
                 copy_w(later).wait_send()
 
-            @pl.when(t < steps - 1)
-            def _():
-                partial_h(later)
-                copy_w(later).start()
+            partial_h(later)
+
+            if last_snapshot:
+
+                @pl.when(before_last)
+                def _():
+                    for part in range(2):
+                        tiny_w[part : part + 1] = row_of(out_w[later, 2 + part], monitor)
+                    copy_tiny_w().start()
+
+            copy_w(later).start()
 
         def inner(x, held):
             e_update(x, drive, get(h_ref, 1, x - 1), get(h_ref, 2, x - 1))
             return held
 
+        for turn in range(min(rounds, steps - 1)):
+
+            @pl.when(t == turn)
+            def _():
+                if turn > 0:
+                    learn(turn - 1)
+                spread(turn)
+
         lax.fori_loop(0, rows - 1, h_plane, 0)
         hx_plane(rows - 1)
+        pl.when(even)(right)
+        pl.when(jnp.logical_not(even))(left)
+        lax.fori_loop(1, rows - 1, inner, 0)
         pl.when(even)(left)
         pl.when(jnp.logical_not(even))(right)
-        lax.fori_loop(1, rows - 1, inner, 0)
 
         @pl.when(snapshot)
         def _():
-            total = lax.fori_loop(1, rows - 1, power, empty)
-            report_ref[pl.ds(lax.div(t, INTERVAL), 1)] = jnp.sum(total, axis=0, keepdims=True)
-
-        pl.when(even)(right)
-        pl.when(jnp.logical_not(even))(left)
-
-        @pl.when(snapshot)
-        def _():
-            total = power(0, power(rows - 1, empty))
-            at = lax.div(t, INTERVAL)
-            report_ref[pl.ds(at, 1)] += jnp.sum(total, axis=0, keepdims=True)
+            note(lax.fori_loop(0, rows, power, empty), lax.div(t, INTERVAL))
 
         return carry
 
-    lax.fori_loop(0, steps, step, 0)
+    lax.fori_loop(0, steps - 1, step, 0)
+    for turn in range(min(rounds, steps - 1), rounds):
+        if turn > 0:
+            learn(turn - 1)
+        spread(turn)
+    if rounds > 0:
+        learn(rounds - 1)
 
     def tell(offset):
         return pltpu.make_async_remote_copy(
@@ -393,25 +490,97 @@
         tell(offset).start()
         return carry
 
+    slot = (steps - 1) % 2
+    drive = wave_ref[steps - 1]
+
+    def inner_power(x, total):
+        e_update(x, drive, get(h_ref, 1, x - 1), get(h_ref, 2, x - 1))
+        return power(x, total)
+
+    lax.fori_loop(0, rows - 1, h_plane, 0)
+    hx_plane(rows - 1)
+    total = lax.fori_loop(1, rows - 1, inner_power, empty)
+    if last_snapshot:
+
+        def unpack(ref, at, z):
+            return tuple(at_lane(ref[at + part : at + part + 1], z) for part in range(2))
+
+        copy_tiny_w().wait_recv()
+        turned = rotate(unpack(got_tiny_w, 0, monitor), start_cos, start_sin)
+        hz_prev = tuple(w + h_gain * e for w, e in zip(turned, get(e_ref, 1, 0)))
+        hx, hy, hz = get(h_ref, 0, 0), get(h_ref, 1, 0), get(h_ref, 2, 0)
+        for value in new_ex(0, drive, hy, hz) + new_ey(0, hx, hz, hz_prev):
+            total = total + value * value
+
+        copy_tiny_e().wait_recv()
+        x = rows - 1
+        beyond_y = rotate(unpack(got_tiny_e, 0, monitor), end_cos, end_sin)
+        beyond_z = plus(unpack(got_tiny_e, 2, monitor), unpack(got_tiny_e, 4, monitor - 1))
+        beyond_z = rotate(beyond_z, end_cos, end_sin)
+        w_y, w_z = get_plane(out_w, slot, 0), get_plane(out_w, slot, 1)
+        hy = tuple(w - h_gain * b for w, b in zip(w_y, beyond_z))
+        hz = tuple(w + h_gain * b for w, b in zip(w_z, beyond_y))
+        hx = get(h_ref, 0, x)
+        for value in new_ex(x, drive, hy, hz) + new_ey(x, hx, hz, get(h_ref, 2, x - 1)):
+            total = total + value * value
+        note(total, steps // INTERVAL - 1)
+
     lax.fori_loop(1, everyone, tell_start, 0)
     got_report[me] = report_ref[...]
-    for t in (steps - 2, steps - 1):
+
+    def last_left():
+        copy_w(slot).wait_recv()
+        e_first(slot, drive)
+
+    def last_right():
+        copy_e(slot).wait_recv()
+        complete_h(slot)
+        e_update(rows - 1, drive, get(h_ref, 1, rows - 2), get(h_ref, 2, rows - 2))
+
+    for side in (last_left, last_right) if slot else (last_right, last_left):
+        side()
+    for t in range(max(steps - 2, 0), steps):
         copy_e(t % 2).wait_send()
         copy_w(t % 2).wait_send()
+    if last_snapshot:
+        copy_tiny_e().wait_send()
+        copy_tiny_w().wait_send()
     everything = got_report.at[pl.ds(0, everyone - 1)]
     pltpu.make_async_copy(everything, everything, recv_report).wait()
     pltpu.make_async_copy(everything, everything, send_report).wait()
 
     def gather(at, held):
-        value = got_report[at]
-        ours = (lax.div(at, slabs) == group).astype(jnp.float32)
-        return held[0] + value, held[1] + ours * value
-
-    zero = jnp.zeros(report_ref.shape, jnp.float32)
-    total, ours = lax.fori_loop(0, everyone, gather, (zero, zero))
+        return held + got_report[group * slabs + at]
+
+    ours = lax.fori_loop(0, slabs, gather, jnp.zeros((1, depth), jnp.float32))
+    total = jnp.sum(got_report[...], axis=0)
     cells = rows * slabs * width
-    reflected_ref[...] = ours / cells
-    mean_ref[...] = total / cells / groups
+    power_ref[0:1] = ours / cells
+    power_ref[1:2] = total / cells / groups
+
+
+def write_out(e_ref, h_ref, power_ref, e_out, h_out, reflected_out, mean_out, own, mean, sems):
+    members = e_ref.shape[1]
+    snaps = mean.shape[0]
+    writes = [
+        pltpu.make_async_copy(src.at[0, member], dst.at[0, member], sems.at[at, member])
+        for at, (src, dst) in enumerate(((e_ref, e_out), (h_ref, h_out)))
+        for member in range(members)
+    ]
+    for write in writes:
+        write.start()
+    lane = lax.broadcasted_iota(jnp.int32, (1, power_ref.shape[1]), 1)
+    for at in range(snaps):
+        own[0, at] = jnp.sum(jnp.where(lane == at, power_ref[0:1], 0.0))
+        mean[at] = jnp.sum(jnp.where(lane == at, power_ref[1:2], 0.0))
+    small = [
+        pltpu.make_async_copy(own, reflected_out, sems.at[0, members]),
+        pltpu.make_async_copy(mean, mean_out, sems.at[1, members]),
+    ]
+    for write in small:
+        write.start()
+    for write in writes + small:
+        write.wait()
 
 
 def one_point(bloch, material, permittivity, peak, sheet, waveform, electric, magnetic):
@@ -419,20 +588,19 @@
     snaps = waveform.shape[0] // INTERVAL
     everyone = lax.axis_size("ka") * lax.axis_size("sp")
     hbm = pl.BlockSpec(memory_space=pltpu.HBM)
-    lines = -(-snaps // 8) * 8
     vmem = pl.BlockSpec(memory_space=pltpu.VMEM)
     plane = (2, 4, width, depth)
     f32 = jnp.float32
-    return pl.pallas_call(
+    tiny = [pltpu.VMEM((rows_of_tiny, width), f32) for rows_of_tiny in (6, 2, 6, 2)]
+    electric_end, magnetic_end, power = pl.pallas_call(
         kernel,
         out_shape=(
             jax.ShapeDtypeStruct(electric.shape, f32),
             jax.ShapeDtypeStruct(magnetic.shape, f32),
-            jax.ShapeDtypeStruct((lines, depth), f32),
-            jax.ShapeDtypeStruct((lines, depth), f32),
+            jax.ShapeDtypeStruct((8, depth), f32),
         ),
         in_specs=[hbm] * 8,
-        out_specs=(vmem, vmem, vmem, vmem),
+        out_specs=(vmem, vmem, vmem),
         scratch_shapes=[
             pltpu.SMEM(bloch.shape, jnp.int32),
             pltpu.SMEM(permittivity.shape, f32),
@@ -442,8 +610,8 @@
             pltpu.VMEM(sheet.shape, f32),
             pltpu.VMEM(electric.shape, electric.dtype),
             pltpu.VMEM(magnetic.shape, magnetic.dtype),
-            pltpu.VMEM((lines, depth), f32),
-            pltpu.VMEM((everyone, lines, depth), f32),
+            pltpu.VMEM((1, depth), f32),
+            pltpu.VMEM((everyone, 1, depth), f32),
             pltpu.VMEM((rows, width, depth), f32),
             pltpu.VMEM((rows, width, depth), f32),
             pltpu.VMEM((2, rows, width, depth), f32),
@@ -451,6 +619,9 @@
             pltpu.VMEM(plane, f32),
             pltpu.VMEM(plane, f32),
             pltpu.VMEM(plane, f32),
+            *tiny,
+            pltpu.SemaphoreType.DMA((2,)),
+            pltpu.SemaphoreType.DMA((2,)),
             pltpu.SemaphoreType.DMA((2,)),
             pltpu.SemaphoreType.DMA((2,)),
             pltpu.SemaphoreType.DMA((2,)),
@@ -458,11 +629,29 @@
             pltpu.SemaphoreType.DMA((12,)),
             pltpu.SemaphoreType.DMA,
             pltpu.SemaphoreType.DMA,
+            pltpu.SemaphoreType.REGULAR((max(everyone.bit_length(), 1),)),
         ],
         compiler_params=pltpu.CompilerParams(
             collective_id=0, has_side_effects=True, vmem_limit_bytes=40 * 1024 * 1024
         ),
     )(*((v if v.shape == (1,) else pltpu.with_memory_space_constraint(v, pltpu.HBM)) for v in (bloch, permittivity, peak, waveform, material, sheet, electric, magnetic)))
+    return pl.pallas_call(
+        write_out,
+        out_shape=(
+            pltpu.HBM(electric.shape, f32),
+            pltpu.HBM(magnetic.shape, f32),
+            pltpu.HBM((1, snaps), f32),
+            pltpu.HBM((snaps,), f32),
+        ),
+        in_specs=[vmem] * 3,
+        out_specs=(hbm,) * 4,
+        scratch_shapes=[
+            pltpu.SMEM((1, snaps), f32),
+            pltpu.SMEM((snaps,), f32),
+            pltpu.SemaphoreType.DMA((2, electric.shape[1] + 1)),
+        ],
+        compiler_params=pltpu.CompilerParams(vmem_limit_bytes=1024 * 1024),
+    )(electric_end, magnetic_end, power)
 
 
 def on_device(
@@ -489,12 +678,15 @@
         )
         for p in range(points)
     ]
-    electric_out = jnp.concatenate([r[0] for r in results], 0)
-    magnetic_out = jnp.concatenate([r[1] for r in results], 0)
-    snaps = waveform.shape[0] // INTERVAL
-    reflected = jnp.stack([r[2][:snaps, PML + 6] for r in results], 0)
-    reflected_mean = sum(r[3][:snaps, PML + 6] for r in results) / points
-    return (electric_out, magnetic_out, reflected, reflected_mean)
+    if points == 1:
+        return results[0]
+    electric_out, magnetic_out, reflected, mean = (list(r) for r in zip(*results))
+    return (
+        jnp.concatenate(electric_out, 0),
+        jnp.concatenate(magnetic_out, 0),
+        jnp.concatenate(reflected, 0),
+        sum(mean) / points,
+    )
 
 
 def solution(mesh):

time: 75.1 us -> 71.2 us (0.948)
  local copies, waits for them, and re-layouts: 4.06 us -> 0 us
    unnamed x2 -> x0, local copies, waits for them, and re-layouts: 3.33 us -> none
    pallas_call x0 -> x1, Pallas kernels: none -> 2.79 us  [one_point(): pl.pallas_call(write_out, out_shape=(pltpu.HBM(electric.shape, f32), pltp...]
    pallas_call x1, Pallas kernels: 69.6 us -> 67 us  [one_point(): pl.pallas_call(kernel, out_shape=(jax.ShapeDtypeStruct(electric.shape, f3...]
where the time goes in v1:
time: 71.2 us; the launch traced here: 71.1 us
  Pallas kernels  69.8 us (98%)
  between operations  1.29 us (2%)
    pallas_call x1, Pallas kernels, one_point(): pl.pallas_call(kernel, out_shape=(jax.ShapeDtypeStruct(electric.shape, f3...  67 us
    pallas_call x1, Pallas kernels, one_point(): pl.pallas_call(write_out, out_shape=(pltpu.HBM(electric.shape, f32), pltp...  2.79 us

profile of v1, /device:TPU:0, one launch (start us, length us, event | category | flops | bytes accessed | tf_op | source)
XLA Modules:
  0.0 71.1 jit_solution(2993900474339522542)
XLA Ops:
  1.3 67.0 %shard_map.111 = (f32[1,6,16,64,128]{4,3,2,1,0:T(8,128)S(1)}, f32[1,6,16,64,128]{4,3,2,1,0:T(8,128)S(1)}, f32[8,128]{1,0:T(8,128)S(1)}) custom-call(s32[1,2]{1,0:T(1,128)} %bloch_in.1, f32[3]{0:T(128)} %perm_in.1, f32[1]{0:T(128)S(6)} %copy.12.peak_in, f32[10]{0:T(128)} %wave_in.1, s32[16,64,128]{2,1,0:T(8,128)} %material_in.1, f32[1,2,16,64]{3,2,1,0:T(8,128)} %sheet_in.1, ...), custom_call_target="tpu_custom_call" | custom-call | tf_op jit(solution)/shard_map/pallas_call | solution.py:595
  68.3 2.8 %shard_map.112 = (f32[1,6,16,64,128]{4,3,2,1,0:T(8,128)}, f32[1,6,16,64,128]{4,3,2,1,0:T(8,128)}, f32[1,2]{1,0:T(1,128)}, f32[2]{0:T(128)}) custom-call(f32[1,6,16,64,128]{4,3,2,1,0:T(8,128)S(1)} %get-tuple-element.7.e_ref, f32[1,6,16,64,128]{4,3,2,1,0:T(8,128)S(1)} %get-tuple-element.8.h_ref, f32[8,128]{1,0:T(8,128)S(1)} %get-tuple-element.9.power_ref), custom_call_target="tpu_custom_call" | custom-call | tf_op jit(solution)/shard_map/pallas_call | solution.py:638

commit v2 on v1

--- a/solution.py
+++ b/solution.py
@@ -58,10 +58,9 @@
     out_w,
     got_e,
     got_w,
-    tiny_e,
-    tiny_w,
-    got_tiny_e,
-    got_tiny_w,
+    tiny,
+    got_tiny,
+    ahead_ref,
     send_e,
     send_w,
     recv_e,
@@ -225,21 +224,26 @@
         ref[slot, 2 * member] = couple[0]
         ref[slot, 2 * member + 1] = couple[1]
 
+    def new_hx(x, ey, ez):
+        change = minus(minus(above_y(ez), ez), minus(above_z(ey), ey))
+        return relax(get(h_ref, 0, x), change, h_keep, h_gain)
+
+    def new_hy(x, ex, ez, ez_next):
+        change = minus(minus(above_z(ex), ex), minus(ez_next, ez))
+        return relax(get(h_ref, 1, x), change, h_keep, h_gain)
+
+    def new_hz(x, ex, ey, ey_next):
+        change = minus(minus(ey_next, ey), minus(above_y(ex), ex))
+        return relax(get(h_ref, 2, x), change, h_keep, h_gain)
+
     def hx_plane(x):
-        ey, ez = get(e_ref, 1, x), get(e_ref, 2, x)
-        change = minus(minus(above_y(ez), ez), minus(above_z(ey), ey))
-        put(h_ref, 0, x, relax(get(h_ref, 0, x), change, h_keep, h_gain))
-
-    def h_plane(x, carry):
-        hx_plane(x)
+        put(h_ref, 0, x, new_hx(x, get(e_ref, 1, x), get(e_ref, 2, x)))
+
+    def h_plane(x):
         ex, ey, ez = get(e_ref, 0, x), get(e_ref, 1, x), get(e_ref, 2, x)
-        dx_ez = minus(get(e_ref, 2, x + 1), ez)
-        dx_ey = minus(get(e_ref, 1, x + 1), ey)
-        change = minus(minus(above_z(ex), ex), dx_ez)
-        put(h_ref, 1, x, relax(get(h_ref, 1, x), change, h_keep, h_gain))
-        change = minus(dx_ey, minus(above_y(ex), ex))
-        put(h_ref, 2, x, relax(get(h_ref, 2, x), change, h_keep, h_gain))
-        return carry
+        put(h_ref, 0, x, new_hx(x, ey, ez))
+        put(h_ref, 1, x, new_hy(x, ex, ez, get(e_ref, 2, x + 1)))
+        put(h_ref, 2, x, new_hz(x, ex, ey, get(e_ref, 1, x + 1)))
 
     def partial_h(slot):
         x = rows - 1
@@ -262,9 +266,9 @@
         change = (change[0] - drive * drive_ref[0, x], change[1] - drive * drive_ref[1, x])
         return relax(get(e_ref, 0, x), change, keep_ref[x], gain_ref[x])
 
-    def new_ey(x, hx, hz, hz_prev):
+    def new_ey(x, ey, hx, hz, hz_prev):
         change = minus(minus(hx, below_z(hx)), minus(hz, hz_prev))
-        return relax(get(e_ref, 1, x), change, keep_ref[x], gain_ref[x])
+        return relax(ey, change, keep_ref[x], gain_ref[x])
 
     def new_ez(x, hx, hy, hy_prev):
         change = minus(minus(hy, hy_prev), minus(hx, below_y(hx)))
@@ -273,19 +277,27 @@
     def e_update(x, drive, hy_prev, hz_prev):
         hx, hy, hz = get(h_ref, 0, x), get(h_ref, 1, x), get(h_ref, 2, x)
         put(e_ref, 0, x, new_ex(x, drive, hy, hz))
-        ey = new_ey(x, hx, hz, hz_prev)
+        ey = new_ey(x, get(e_ref, 1, x), hx, hz, hz_prev)
         put(e_ref, 1, x, ey)
         ez = new_ez(x, hx, hy, hy_prev)
         put(e_ref, 2, x, ez)
         return ey, ez
 
-    def e_first(slot, drive):
-        ey, ez = get(e_ref, 1, 0), get(e_ref, 2, 0)
+    def beside(turned_y, turned_z, ey, ez):
+        hy_prev = tuple(w - h_gain * e for w, e in zip(turned_y, ez))
+        hz_prev = tuple(w + h_gain * e for w, e in zip(turned_z, ey))
+        return hy_prev, hz_prev
+
+    def got_beside(slot):
         turned_y = rotate(get_plane(got_w, slot, 0), start_cos, start_sin)
         turned_z = rotate(get_plane(got_w, slot, 1), start_cos, start_sin)
-        hy_prev = tuple(w - h_gain * e for w, e in zip(turned_y, ez))
-        hz_prev = tuple(w + h_gain * e for w, e in zip(turned_z, ey))
-        return e_update(0, drive, hy_prev, hz_prev)
+        return beside(turned_y, turned_z, get(e_ref, 1, 0), get(e_ref, 2, 0))
+
+    def e_first(slot, drive):
+        return e_update(0, drive, *got_beside(slot))
+
+    def e_middle(x, drive):
+        return e_update(x, drive, get(h_ref, 1, x - 1), get(h_ref, 2, x - 1))
 
     def copy_e(slot):
         return pltpu.make_async_remote_copy(
@@ -320,21 +332,27 @@
         column = jnp.sum(jnp.where(square, row, 0.0), axis=1, keepdims=True)
         return jnp.where(lane == z, column, 0.0)
 
-    def copy_tiny(src, dst, at, other):
+    def copy_tiny(at, other):
         return pltpu.make_async_remote_copy(
-            src_ref=src,
-            dst_ref=dst,
+            src_ref=tiny.at[at],
+            dst_ref=got_tiny.at[at],
             send_sem=send_tiny.at[at],
             recv_sem=recv_tiny.at[at],
             device_id={"sp": other},
             device_id_type=MESH,
         )
 
-    def copy_tiny_e():
-        return copy_tiny(tiny_e, got_tiny_e, 0, lower)
-
-    def copy_tiny_w():
-        return copy_tiny(tiny_w, got_tiny_w, 1, upper)
+    def pack(at, columns):
+        for place_in, (couple, z) in enumerate(columns):
+            for part in range(2):
+                line = 2 * place_in + part
+                tiny[at, line : line + 1] = row_of(couple[part], z)
+
+    def unpack(at, place_in, z):
+        lines = (2 * place_in, 2 * place_in + 1)
+        return tuple(at_lane(got_tiny[at, line : line + 1], z) for line in lines)
+
+    early_w, late_w, late_e = (copy_tiny(0, upper), copy_tiny(1, upper), copy_tiny(2, lower))
 
     def widen(x, carry):
         for member in range(6):
@@ -383,70 +401,75 @@
 
     row_lane = lax.broadcasted_iota(jnp.int32, (1, depth), 1)
     empty = jnp.zeros((width, depth), jnp.float32)
-    last_snapshot = steps % INTERVAL == 0
+    assert steps % (2 * INTERVAL) == 0
 
     def note(total, at):
         amount = jnp.sum(jnp.where(lane == monitor, total, 0.0), axis=0, keepdims=True)
         amount = jnp.sum(amount, axis=1, keepdims=True)
         report_ref[...] += jnp.where(row_lane == at, amount, 0.0)
+
+    def sides(t, slot, later, drive):
+        def left():
+            copy_w(slot).wait_recv()
+            ey, ez = e_first(slot, drive)
+
+            @pl.when(t >= 1)
+            def _():
+                copy_e(later).wait_send()
+
+            put_plane(out_e, later, 0, ey)
+            put_plane(out_e, later, 1, ez)
+            copy_e(later).start()
+
+        def right():
+            copy_e(slot).wait_recv()
+            complete_h(slot)
+            e_middle(rows - 1, drive)
+
+            @pl.when(t >= 1)
+            def _():
+                copy_w(later).wait_send()
+
+            partial_h(later)
+
+            @pl.when(t == steps - 3)
+            def _():
+                w_y, w_z = get_plane(out_w, later, 0), get_plane(out_w, later, 1)
+                pack(
+                    0,
+                    [(w_z, monitor - 1), (w_z, monitor), (w_z, monitor + 1)]
+                    + [(w_y, monitor - 1), (w_y, monitor)],
+                )
+                early_w.start()
+
+            copy_w(later).start()
+
+        return left, right
+
+    def before_sides():
+        h_plane(0)
+        h_plane(1)
+        h_plane(rows - 2)
+        hx_plane(rows - 1)
+
+    def between_sides(drive):
+        def both(x, held):
+            e_middle(x, drive)
+            h_plane(x + 1)
+            return held
+
+        lax.fori_loop(1, rows - 3, both, 0)
+        e_middle(rows - 3, drive)
+        e_middle(rows - 2, drive)
 
     def step(t, carry):
         slot = lax.rem(t, 2)
         later = lax.rem(t + 1, 2)
         drive = wave_ref[t]
         even = slot == 0
-        snapshot = lax.rem(t + 1, INTERVAL) == 0
-        before_last = t == steps - 2
-
-        def left():
-            copy_w(slot).wait_recv()
-            ey, ez = e_first(slot, drive)
-
-            @pl.when(t >= 1)
-            def _():
-                copy_e(later).wait_send()
-
-            put_plane(out_e, later, 0, ey)
-            put_plane(out_e, later, 1, ez)
-
-            if last_snapshot:
-
-                @pl.when(before_last)
-                def _():
-                    for part in range(2):
-                        tiny_e[part : part + 1] = row_of(ey[part], monitor)
-                        tiny_e[2 + part : 3 + part] = row_of(ez[part], monitor)
-                        tiny_e[4 + part : 5 + part] = row_of(ez[part], monitor - 1)
-                    copy_tiny_e().start()
-
-            copy_e(later).start()
-
-        def right():
-            copy_e(slot).wait_recv()
-            complete_h(slot)
-            e_update(rows - 1, drive, get(h_ref, 1, rows - 2), get(h_ref, 2, rows - 2))
-
-            @pl.when(t >= 1)
-            def _():
-                copy_w(later).wait_send()
-
-            partial_h(later)
-
-            if last_snapshot:
-
-                @pl.when(before_last)
-                def _():
-                    for part in range(2):
-                        tiny_w[part : part + 1] = row_of(out_w[later, 2 + part], monitor)
-                    copy_tiny_w().start()
-
-            copy_w(later).start()
-
-        def inner(x, held):
-            e_update(x, drive, get(h_ref, 1, x - 1), get(h_ref, 2, x - 1))
-            return held
-
-        for turn in range(min(rounds, steps - 1)):
+        left, right = sides(t, slot, later, drive)
+
+        for turn in range(min(rounds, steps - 2)):
 
             @pl.when(t == turn)
             def _():
@@ -454,22 +477,21 @@
                     learn(turn - 1)
                 spread(turn)
 
-        lax.fori_loop(0, rows - 1, h_plane, 0)
-        hx_plane(rows - 1)
+        before_sides()
         pl.when(even)(right)
         pl.when(jnp.logical_not(even))(left)
-        lax.fori_loop(1, rows - 1, inner, 0)
+        between_sides(drive)
         pl.when(even)(left)
         pl.when(jnp.logical_not(even))(right)
 
-        @pl.when(snapshot)
+        @pl.when(lax.rem(t + 1, INTERVAL) == 0)
         def _():
             note(lax.fori_loop(0, rows, power, empty), lax.div(t, INTERVAL))
 
         return carry
 
-    lax.fori_loop(0, steps - 1, step, 0)
-    for turn in range(min(rounds, steps - 1), rounds):
+    lax.fori_loop(0, steps - 2, step, 0)
+    for turn in range(min(rounds, steps - 2), rounds):
         if turn > 0:
             learn(turn - 1)
         spread(turn)
@@ -490,61 +512,106 @@
         tell(offset).start()
         return carry
 
-    slot = (steps - 1) % 2
-    drive = wave_ref[steps - 1]
-
-    def inner_power(x, total):
-        e_update(x, drive, get(h_ref, 1, x - 1), get(h_ref, 2, x - 1))
+    slot, later = (steps - 2) % 2, (steps - 1) % 2
+    drive, last_drive = wave_ref[steps - 2], wave_ref[steps - 1]
+    end = rows - 1
+    before_sides()
+    between_sides(drive)
+    early_w.wait_recv()
+    hx, hy, hz = get(h_ref, 0, 0), get(h_ref, 1, 0), get(h_ref, 2, 0)
+    put(e_ref, 0, 0, new_ex(0, drive, hy, hz))
+    w_z = plus(plus(unpack(0, 0, monitor - 1), unpack(0, 1, monitor)), unpack(0, 2, monitor + 1))
+    w_y = plus(unpack(0, 3, monitor - 1), unpack(0, 4, monitor))
+    ey, ez = get(e_ref, 1, 0), get(e_ref, 2, 0)
+    hy_prev, hz_prev = beside(
+        rotate(w_y, start_cos, start_sin), rotate(w_z, start_cos, start_sin), ey, ez
+    )
+    ey = new_ey(0, ey, hx, hz, hz_prev)
+    ez = new_ez(0, hx, hy, hy_prev)
+    put_plane(ahead_ref, 0, 0, ey)
+    put_plane(ahead_ref, 0, 1, ez)
+    pack(2, [(ey, monitor), (ez, monitor), (ez, monitor - 1)])
+    late_e.start()
+
+    copy_e(slot).wait_recv()
+    complete_h(slot)
+    e_middle(end, drive)
+    copy_w(later).wait_send()
+    partial_h(later)
+    pack(1, [(get_plane(out_w, later, 1), monitor)])
+    late_w.start()
+    copy_w(later).start()
+
+    h_plane(1)
+    h_plane(2)
+
+    def both(x, total):
+        e_middle(x, last_drive)
+        h_plane(x + 1)
         return power(x, total)
 
-    lax.fori_loop(0, rows - 1, h_plane, 0)
-    hx_plane(rows - 1)
-    total = lax.fori_loop(1, rows - 1, inner_power, empty)
-    if last_snapshot:
-
-        def unpack(ref, at, z):
-            return tuple(at_lane(ref[at + part : at + part + 1], z) for part in range(2))
-
-        copy_tiny_w().wait_recv()
-        turned = rotate(unpack(got_tiny_w, 0, monitor), start_cos, start_sin)
-        hz_prev = tuple(w + h_gain * e for w, e in zip(turned, get(e_ref, 1, 0)))
+    total = lax.fori_loop(2, end - 1, both, empty)
+    e_middle(end - 1, last_drive)
+    total = power(end - 1, total)
+    hx_plane(end)
+
+    def first_plane():
+        copy_w(slot).wait_recv()
         hx, hy, hz = get(h_ref, 0, 0), get(h_ref, 1, 0), get(h_ref, 2, 0)
-        for value in new_ex(0, drive, hy, hz) + new_ey(0, hx, hz, hz_prev):
-            total = total + value * value
-
-        copy_tiny_e().wait_recv()
-        x = rows - 1
-        beyond_y = rotate(unpack(got_tiny_e, 0, monitor), end_cos, end_sin)
-        beyond_z = plus(unpack(got_tiny_e, 2, monitor), unpack(got_tiny_e, 4, monitor - 1))
-        beyond_z = rotate(beyond_z, end_cos, end_sin)
-        w_y, w_z = get_plane(out_w, slot, 0), get_plane(out_w, slot, 1)
-        hy = tuple(w - h_gain * b for w, b in zip(w_y, beyond_z))
-        hz = tuple(w + h_gain * b for w, b in zip(w_z, beyond_y))
-        hx = get(h_ref, 0, x)
-        for value in new_ex(x, drive, hy, hz) + new_ey(x, hx, hz, get(h_ref, 2, x - 1)):
-            total = total + value * value
-        note(total, steps // INTERVAL - 1)
-
+        hy_prev, hz_prev = got_beside(slot)
+        ey = new_ey(0, get(e_ref, 1, 0), hx, hz, hz_prev)
+        ez = new_ez(0, hx, hy, hy_prev)
+        put(e_ref, 1, 0, ey)
+        put(e_ref, 2, 0, ez)
+        copy_e(later).wait_send()
+        put_plane(out_e, later, 0, ey)
+        put_plane(out_e, later, 1, ez)
+        copy_e(later).start()
+
+    first_plane()
+    ex, ey, ez = get(e_ref, 0, 0), get_plane(ahead_ref, 0, 0), get_plane(ahead_ref, 0, 1)
+    hx = new_hx(0, ey, ez)
+    hy = new_hy(0, ex, ez, get(e_ref, 2, 1))
+    hz = new_hz(0, ex, ey, get(e_ref, 1, 1))
+    hx1, hy1, hz1 = get(h_ref, 0, 1), get(h_ref, 1, 1), get(h_ref, 2, 1)
+    late_w.wait_recv()
+    hz_prev = rotate(unpack(1, 0, monitor), start_cos, start_sin)
+    hz_prev = tuple(w + h_gain * e for w, e in zip(hz_prev, ey))
+    for value in (
+        new_ex(0, last_drive, hy, hz)
+        + new_ey(0, ey, hx, hz, hz_prev)
+        + new_ex(1, last_drive, hy1, hz1)
+        + new_ey(1, get(e_ref, 1, 1), hx1, hz1, hz)
+    ):
+        total = total + value * value
+    late_e.wait_recv()
+    beyond_y = rotate(unpack(2, 0, monitor), end_cos, end_sin)
+    beyond_z = plus(unpack(2, 1, monitor), unpack(2, 2, monitor - 1))
+    beyond_z = rotate(beyond_z, end_cos, end_sin)
+    w_y, w_z = get_plane(out_w, later, 0), get_plane(out_w, later, 1)
+    hx = get(h_ref, 0, end)
+    hy = tuple(w - h_gain * b for w, b in zip(w_y, beyond_z))
+    hz = tuple(w + h_gain * b for w, b in zip(w_z, beyond_y))
+    for value in new_ex(end, last_drive, hy, hz) + new_ey(
+        end, get(e_ref, 1, end), hx, hz, get(h_ref, 2, end - 1)
+    ):
+        total = total + value * value
+    note(total, steps // INTERVAL - 1)
     lax.fori_loop(1, everyone, tell_start, 0)
     got_report[me] = report_ref[...]
 
-    def last_left():
-        copy_w(slot).wait_recv()
-        e_first(slot, drive)
-
-    def last_right():
-        copy_e(slot).wait_recv()
-        complete_h(slot)
-        e_update(rows - 1, drive, get(h_ref, 1, rows - 2), get(h_ref, 2, rows - 2))
-
-    for side in (last_left, last_right) if slot else (last_right, last_left):
-        side()
-    for t in range(max(steps - 2, 0), steps):
-        copy_e(t % 2).wait_send()
-        copy_w(t % 2).wait_send()
-    if last_snapshot:
-        copy_tiny_e().wait_send()
-        copy_tiny_w().wait_send()
+    h_plane(0)
+    e_middle(1, last_drive)
+    copy_w(later).wait_recv()
+    e_first(later, last_drive)
+    copy_e(later).wait_recv()
+    complete_h(later)
+    e_middle(end, last_drive)
+    for at in range(2):
+        copy_e(at).wait_send()
+        copy_w(at).wait_send()
+    for copy in (early_w, late_w, late_e):
+        copy.wait_send()
     everything = got_report.at[pl.ds(0, everyone - 1)]
     pltpu.make_async_copy(everything, everything, recv_report).wait()
     pltpu.make_async_copy(everything, everything, send_report).wait()
@@ -591,7 +658,6 @@
     vmem = pl.BlockSpec(memory_space=pltpu.VMEM)
     plane = (2, 4, width, depth)
     f32 = jnp.float32
-    tiny = [pltpu.VMEM((rows_of_tiny, width), f32) for rows_of_tiny in (6, 2, 6, 2)]
     electric_end, magnetic_end, power = pl.pallas_call(
         kernel,
         out_shape=(
@@ -619,13 +685,15 @@
             pltpu.VMEM(plane, f32),
             pltpu.VMEM(plane, f32),
             pltpu.VMEM(plane, f32),
-            *tiny,
+            pltpu.VMEM((3, 16, width), f32),
+            pltpu.VMEM((3, 16, width), f32),
+            pltpu.VMEM((1, 4, width, depth), f32),
             pltpu.SemaphoreType.DMA((2,)),
             pltpu.SemaphoreType.DMA((2,)),
             pltpu.SemaphoreType.DMA((2,)),
             pltpu.SemaphoreType.DMA((2,)),
-            pltpu.SemaphoreType.DMA((2,)),
-            pltpu.SemaphoreType.DMA((2,)),
+            pltpu.SemaphoreType.DMA((3,)),
+            pltpu.SemaphoreType.DMA((3,)),
             pltpu.SemaphoreType.DMA((12,)),
             pltpu.SemaphoreType.DMA,
             pltpu.SemaphoreType.DMA,

time: 71.2 us -> 68.5 us (0.962)
  Pallas kernels: 69.8 us -> 67.1 us
    pallas_call x1, Pallas kernels: 67 us -> 64.3 us  [one_point(): pl.pallas_call(kernel, out_shape=(jax.ShapeDtypeStruct(electric.shape, f3...]
where the time goes in v2:
time: 68.5 us; the launch traced here: 68.4 us
  Pallas kernels  67.1 us (98%)
  between operations  1.29 us (2%)
    pallas_call x1, Pallas kernels, one_point(): pl.pallas_call(kernel, out_shape=(jax.ShapeDtypeStruct(electric.shape, f3...  64.3 us
    pallas_call x1, Pallas kernels, one_point(): pl.pallas_call(write_out, out_shape=(pltpu.HBM(electric.shape, f32), pltp...  2.79 us

profile of v2, /device:TPU:0, one launch (start us, length us, event | category | flops | bytes accessed | tf_op | source)
XLA Modules:
  0.0 68.4 jit_solution(14678877903174381596)
XLA Ops:
  1.3 64.3 %shard_map.111 = (f32[1,6,16,64,128]{4,3,2,1,0:T(8,128)S(1)}, f32[1,6,16,64,128]{4,3,2,1,0:T(8,128)S(1)}, f32[8,128]{1,0:T(8,128)S(1)}) custom-call(s32[1,2]{1,0:T(1,128)} %bloch_in.1, f32[3]{0:T(128)} %perm_in.1, f32[1]{0:T(128)S(6)} %copy.12.peak_in, f32[10]{0:T(128)} %wave_in.1, s32[16,64,128]{2,1,0:T(8,128)} %material_in.1, f32[1,2,16,64]{3,2,1,0:T(8,128)} %sheet_in.1, ...), custom_call_target="tpu_custom_call" | custom-call | tf_op jit(solution)/shard_map/pallas_call | solution.py:661
  65.6 2.8 %shard_map.112 = (f32[1,6,16,64,128]{4,3,2,1,0:T(8,128)}, f32[1,6,16,64,128]{4,3,2,1,0:T(8,128)}, f32[1,2]{1,0:T(1,128)}, f32[2]{0:T(128)}) custom-call(f32[1,6,16,64,128]{4,3,2,1,0:T(8,128)S(1)} %get-tuple-element.7.e_ref, f32[1,6,16,64,128]{4,3,2,1,0:T(8,128)S(1)} %get-tuple-element.8.h_ref, f32[8,128]{1,0:T(8,128)S(1)} %get-tuple-element.9.power_ref), custom_call_target="tpu_custom_call" | custom-call | tf_op jit(solution)/shard_map/pallas_call | solution.py:706

commit v3 on v2

--- a/solution.py
+++ b/solution.py
@@ -115,34 +115,66 @@
     def greet(other):
         pl.semaphore_signal(barrier, inc=1, device_id=place(other), device_id_type=MESH)
 
-    bits = everyone.bit_length() - 1
-    hypercube = everyone == 1 << bits
-    rounds = bits - 1 if hypercube else 0
-    greeted = bits + 2 if hypercube else everyone - 1
-
-    def partner(bit):
-        return me + (1 << bit) * (1 - 2 * lax.rem(lax.div(me, 1 << bit), 2))
-
-    if hypercube:
-        greet(group * slabs + lower)
-        greet(group * slabs + upper)
-        for bit in range(bits):
-            greet(partner(bit))
+    grid = groups % 4 == 0
+    ahead_of = [("flip", 1), ("flip", 2)]
+    stride = 1
+    while stride < groups // 4 - 1:
+        ahead_of.insert(0, ("line", 4 * stride))
+        stride *= 2
+    ahead_of = sorted(ahead_of[:-2], key=lambda turn: turn[1]) + ahead_of[-2:]
+    stride = 1
+    while stride < slabs // 2:
+        ahead_of.append(("ring", stride))
+        stride *= 2
+    rounds = len(ahead_of) if grid else 0
+
+    def peers(kind, stride):
+        if kind == "flip":
+            return [((group + stride * (1 - 2 * lax.rem(lax.div(group, stride), 2))) * slabs + slab, None)]
+        if kind == "ring":
+            return [
+                (group * slabs + lax.rem(slab + stride, slabs), None),
+                (group * slabs + lax.rem(slab + slabs - stride, slabs), None),
+            ]
+        return [
+            ((group + stride) * slabs + slab, group + stride < groups),
+            ((group - stride) * slabs + slab, group >= stride),
+        ]
+
+    def signal_to(semaphore, found):
+        for other, exists in found:
+
+            def signal():
+                pl.semaphore_signal(
+                    semaphore, inc=1, device_id=place(other), device_id_type=MESH
+                )
+
+            if exists is None:
+                signal()
+            else:
+                pl.when(exists)(signal)
+
+    def amount(found):
+        return sum(1 if exists is None else exists.astype(jnp.int32) for _, exists in found)
+
+    if grid:
+        nearest = peers("ring", 1) + peers("flip", 1) + peers("flip", 2) + peers("line", 4)
+        signal_to(barrier, nearest)
+        greeted = amount(nearest)
     else:
 
         def greet_at(offset, carry):
-            greet(lax.rem(me + offset, everyone))
+            signal_to(barrier, [(lax.rem(me + offset, everyone), None)])
             return carry
 
         lax.fori_loop(1, everyone, greet_at, 0)
+        greeted = everyone - 1
 
     def spread(turn):
-        pl.semaphore_signal(
-            entered.at[turn], inc=1, device_id=place(partner(turn)), device_id_type=MESH
-        )
+        signal_to(entered.at[turn], peers(*ahead_of[turn]))
 
     def learn(turn):
-        pl.semaphore_wait(entered.at[turn], 1)
+        pl.semaphore_wait(entered.at[turn], amount(peers(*ahead_of[turn])))
 
     for load in loads[4:8]:
         load.wait()
@@ -245,21 +277,35 @@
         put(h_ref, 1, x, new_hy(x, ex, ez, get(e_ref, 2, x + 1)))
         put(h_ref, 2, x, new_hz(x, ex, ey, get(e_ref, 1, x + 1)))
 
-    def partial_h(slot):
+    def part_y(ex, ez, hy):
+        return relax(hy, plus(minus(above_z(ex), ex), ez), h_keep, h_gain)
+
+    def part_z(ex, ey, hz):
+        return relax(hz, minus(minus(ex, above_y(ex)), ey), h_keep, h_gain)
+
+    def partial_y(slot):
         x = rows - 1
-        ex, ey, ez = get(e_ref, 0, x), get(e_ref, 1, x), get(e_ref, 2, x)
-        change = plus(minus(above_z(ex), ex), ez)
-        put_plane(out_w, slot, 0, relax(get(h_ref, 1, x), change, h_keep, h_gain))
-        change = minus(minus(ex, above_y(ex)), ey)
-        put_plane(out_w, slot, 1, relax(get(h_ref, 2, x), change, h_keep, h_gain))
-
-    def complete_h(slot):
+        put_plane(out_w, slot, 0, part_y(get(e_ref, 0, x), get(e_ref, 2, x), get(h_ref, 1, x)))
+
+    def partial_z(slot):
         x = rows - 1
-        beyond_y = rotate(get_plane(got_e, slot, 0), end_cos, end_sin)
-        beyond_z = rotate(get_plane(got_e, slot, 1), end_cos, end_sin)
-        w_y, w_z = get_plane(out_w, slot, 0), get_plane(out_w, slot, 1)
-        put(h_ref, 1, x, tuple(w - h_gain * b for w, b in zip(w_y, beyond_z)))
-        put(h_ref, 2, x, tuple(w + h_gain * b for w, b in zip(w_z, beyond_y)))
+        put_plane(out_w, slot, 1, part_z(get(e_ref, 0, x), get(e_ref, 1, x), get(h_ref, 2, x)))
+
+    def whole_hz(slot, beyond_y):
+        beyond_y = rotate(beyond_y, end_cos, end_sin)
+        return tuple(w + h_gain * b for w, b in zip(get_plane(out_w, slot, 1), beyond_y))
+
+    def whole_hy(slot, beyond_z):
+        beyond_z = rotate(beyond_z, end_cos, end_sin)
+        return tuple(w - h_gain * b for w, b in zip(get_plane(out_w, slot, 0), beyond_z))
+
+    def hz_below(w_z, ey):
+        turned = rotate(w_z, start_cos, start_sin)
+        return tuple(w + h_gain * e for w, e in zip(turned, ey))
+
+    def hy_below(w_y, ez):
+        turned = rotate(w_y, start_cos, start_sin)
+        return tuple(w - h_gain * e for w, e in zip(turned, ez))
 
     def new_ex(x, drive, hy, hz):
         change = minus(minus(hz, below_y(hz)), minus(hy, below_z(hy)))
@@ -283,38 +329,25 @@
         put(e_ref, 2, x, ez)
         return ey, ez
 
-    def beside(turned_y, turned_z, ey, ez):
-        hy_prev = tuple(w - h_gain * e for w, e in zip(turned_y, ez))
-        hz_prev = tuple(w + h_gain * e for w, e in zip(turned_z, ey))
-        return hy_prev, hz_prev
-
-    def got_beside(slot):
-        turned_y = rotate(get_plane(got_w, slot, 0), start_cos, start_sin)
-        turned_z = rotate(get_plane(got_w, slot, 1), start_cos, start_sin)
-        return beside(turned_y, turned_z, get(e_ref, 1, 0), get(e_ref, 2, 0))
-
-    def e_first(slot, drive):
-        return e_update(0, drive, *got_beside(slot))
-
     def e_middle(x, drive):
         return e_update(x, drive, get(h_ref, 1, x - 1), get(h_ref, 2, x - 1))
 
-    def copy_e(slot):
+    def copy_e(slot, member):
         return pltpu.make_async_remote_copy(
-            src_ref=out_e.at[slot],
-            dst_ref=got_e.at[slot],
-            send_sem=send_e.at[slot],
-            recv_sem=recv_e.at[slot],
+            src_ref=out_e.at[slot, pl.ds(2 * member, 2)],
+            dst_ref=got_e.at[slot, pl.ds(2 * member, 2)],
+            send_sem=send_e.at[slot, member],
+            recv_sem=recv_e.at[slot, member],
             device_id={"sp": lower},
             device_id_type=MESH,
         )
 
-    def copy_w(slot):
+    def copy_w(slot, member):
         return pltpu.make_async_remote_copy(
-            src_ref=out_w.at[slot],
-            dst_ref=got_w.at[slot],
-            send_sem=send_w.at[slot],
-            recv_sem=recv_w.at[slot],
+            src_ref=out_w.at[slot, pl.ds(2 * member, 2)],
+            dst_ref=got_w.at[slot, pl.ds(2 * member, 2)],
+            send_sem=send_w.at[slot, member],
+            recv_sem=recv_w.at[slot, member],
             device_id={"sp": upper},
             device_id_type=MESH,
         )
@@ -323,14 +356,7 @@
         jnp.int32, (width, width), 1
     )
     monitor = PML + 6
-
-    def row_of(value, z):
-        column = jnp.sum(jnp.where(lane == z, value, 0.0), axis=1, keepdims=True)
-        return jnp.sum(jnp.where(square, column, 0.0), axis=0, keepdims=True)
-
-    def at_lane(row, z):
-        column = jnp.sum(jnp.where(square, row, 0.0), axis=1, keepdims=True)
-        return jnp.where(lane == z, column, 0.0)
+    band = monitor // 8 * 8
 
     def copy_tiny(at, other):
         return pltpu.make_async_remote_copy(
@@ -342,17 +368,17 @@
             device_id_type=MESH,
         )
 
-    def pack(at, columns):
-        for place_in, (couple, z) in enumerate(columns):
-            for part in range(2):
-                line = 2 * place_in + part
-                tiny[at, line : line + 1] = row_of(couple[part], z)
-
-    def unpack(at, place_in, z):
-        lines = (2 * place_in, 2 * place_in + 1)
-        return tuple(at_lane(got_tiny[at, line : line + 1], z) for line in lines)
-
-    early_w, late_w, late_e = (copy_tiny(0, upper), copy_tiny(1, upper), copy_tiny(2, lower))
+    def pack(at, member, couple):
+        tiny[at, member] = jnp.concatenate(couple, axis=0).T[band : band + 8]
+
+    def unpack(at, member):
+        before = jnp.zeros((band, 2 * width), jnp.float32)
+        after = jnp.zeros((depth - band - 8, 2 * width), jnp.float32)
+        tall = jnp.concatenate([before, got_tiny[at, member], after], axis=0).T
+        return tall[:width], tall[width:]
+
+    ahead_e1, ahead_e2, ahead_e3 = (copy_tiny(at, lower) for at in range(3))
+    ahead_w2, ahead_w3 = (copy_tiny(at, upper) for at in range(3, 5))
 
     def widen(x, carry):
         for member in range(6):
@@ -364,12 +390,15 @@
     for member in range(4):
         out_e[0, member] = e_in[0, 2 + member, 0].astype(jnp.float32)
     pl.semaphore_wait(barrier, greeted)
-    copy_e(0).start()
+    copy_e(0, 0).start()
+    copy_e(0, 1).start()
     for load in loads[1:4]:
         load.wait()
     widen(rows - 1, 0)
-    partial_h(0)
-    copy_w(0).start()
+    partial_z(0)
+    copy_w(0, 1).start()
+    partial_y(0)
+    copy_w(0, 0).start()
     widen(0, 0)
     for load in loads[8:]:
         load.wait()
@@ -401,48 +430,98 @@
 
     row_lane = lax.broadcasted_iota(jnp.int32, (1, depth), 1)
     empty = jnp.zeros((width, depth), jnp.float32)
-    assert steps % (2 * INTERVAL) == 0
+    assert steps % (2 * INTERVAL) == 0 and rows > 6
 
     def note(total, at):
         amount = jnp.sum(jnp.where(lane == monitor, total, 0.0), axis=0, keepdims=True)
         amount = jnp.sum(amount, axis=1, keepdims=True)
         report_ref[...] += jnp.where(row_lane == at, amount, 0.0)
 
+    def first_y(slot, later, sent, go):
+        copy_w(slot, 1).wait_recv()
+        ey = get(e_ref, 1, 0)
+        hz_prev = hz_below(get_plane(got_w, slot, 1), ey)
+        ey = new_ey(0, ey, get(h_ref, 0, 0), get(h_ref, 2, 0), hz_prev)
+        put(e_ref, 1, 0, ey)
+        if go:
+            pl.when(sent)(lambda: copy_e(later, 0).wait_send())
+            put_plane(out_e, later, 0, ey)
+            copy_e(later, 0).start()
+
+    def first_z(slot, later, sent, go):
+        copy_w(slot, 0).wait_recv()
+        hy_prev = hy_below(get_plane(got_w, slot, 0), get(e_ref, 2, 0))
+        ez = new_ez(0, get(h_ref, 0, 0), get(h_ref, 1, 0), hy_prev)
+        put(e_ref, 2, 0, ez)
+        if go:
+            pl.when(sent)(lambda: copy_e(later, 1).wait_send())
+            put_plane(out_e, later, 1, ez)
+            copy_e(later, 1).start()
+
+    def first_yz_ahead(slot, later, at, copy):
+        first_y(slot, later, True, False)
+        first_z(slot, later, True, False)
+        send_columns(at, copy)
+        for member in range(2):
+            copy_e(later, member).wait_send()
+            put_plane(out_e, later, member, get(e_ref, 1 + member, 0))
+            copy_e(later, member).start()
+
+    def send_columns(at, copy):
+        pack(at, 0, get(e_ref, 1, 0))
+        pack(at, 1, get(e_ref, 2, 0))
+        copy.start()
+
+    def first_x(drive):
+        put(e_ref, 0, 0, new_ex(0, drive, get(h_ref, 1, 0), get(h_ref, 2, 0)))
+
+    def end_fields(slot, drive):
+        x = rows - 1
+        copy_e(slot, 0).wait_recv()
+        hz = whole_hz(slot, get_plane(got_e, slot, 0))
+        put(h_ref, 2, x, hz)
+        hx = get(h_ref, 0, x)
+        put(e_ref, 1, x, new_ey(x, get(e_ref, 1, x), hx, hz, get(h_ref, 2, x - 1)))
+        copy_e(slot, 1).wait_recv()
+        hy = whole_hy(slot, get_plane(got_e, slot, 1))
+        put(h_ref, 1, x, hy)
+        put(e_ref, 0, x, new_ex(x, drive, hy, get(h_ref, 2, x)))
+        put(e_ref, 2, x, new_ez(x, get(h_ref, 0, x), hy, get(h_ref, 1, x - 1)))
+
+    def give_w(later):
+        copy_w(later, 1).wait_send()
+        copy_w(later, 0).wait_send()
+        partial_z(later)
+        copy_w(later, 1).start()
+        partial_y(later)
+        copy_w(later, 0).start()
+
     def sides(t, slot, later, drive):
         def left():
-            copy_w(slot).wait_recv()
-            ey, ez = e_first(slot, drive)
+            first_x(drive)
+            ahead = t == steps - 4
+
+            @pl.when(ahead)
+            def _():
+                first_yz_ahead(slot, later, 0, ahead_e1)
+
+            @pl.when(jnp.logical_not(ahead))
+            def _():
+                first_y(slot, later, t >= 1, True)
+                first_z(slot, later, t >= 1, True)
+
+        def right():
+            end_fields(slot, drive)
 
             @pl.when(t >= 1)
             def _():
-                copy_e(later).wait_send()
-
-            put_plane(out_e, later, 0, ey)
-            put_plane(out_e, later, 1, ez)
-            copy_e(later).start()
-
-        def right():
-            copy_e(slot).wait_recv()
-            complete_h(slot)
-            e_middle(rows - 1, drive)
-
-            @pl.when(t >= 1)
-            def _():
-                copy_w(later).wait_send()
-
-            partial_h(later)
-
-            @pl.when(t == steps - 3)
-            def _():
-                w_y, w_z = get_plane(out_w, later, 0), get_plane(out_w, later, 1)
-                pack(
-                    0,
-                    [(w_z, monitor - 1), (w_z, monitor), (w_z, monitor + 1)]
-                    + [(w_y, monitor - 1), (w_y, monitor)],
-                )
-                early_w.start()
-
-            copy_w(later).start()
+                copy_w(later, 1).wait_send()
+                copy_w(later, 0).wait_send()
+
+            partial_z(later)
+            copy_w(later, 1).start()
+            partial_y(later)
+            copy_w(later, 0).start()
 
         return left, right
 
@@ -469,7 +548,7 @@
         even = slot == 0
         left, right = sides(t, slot, later, drive)
 
-        for turn in range(min(rounds, steps - 2)):
+        for turn in range(min(rounds, steps - 3)):
 
             @pl.when(t == turn)
             def _():
@@ -490,8 +569,8 @@
 
         return carry
 
-    lax.fori_loop(0, steps - 2, step, 0)
-    for turn in range(min(rounds, steps - 2), rounds):
+    lax.fori_loop(0, steps - 3, step, 0)
+    for turn in range(min(rounds, steps - 3), rounds):
         if turn > 0:
             learn(turn - 1)
         spread(turn)
@@ -512,71 +591,92 @@
         tell(offset).start()
         return carry
 
-    slot, later = (steps - 2) % 2, (steps - 1) % 2
-    drive, last_drive = wave_ref[steps - 2], wave_ref[steps - 1]
     end = rows - 1
+    one, two, three = ((steps - 3 + at) % 2 for at in range(3))
+    drive_one, drive, last_drive = (wave_ref[steps - 3 + at] for at in range(3))
     before_sides()
-    between_sides(drive)
-    early_w.wait_recv()
-    hx, hy, hz = get(h_ref, 0, 0), get(h_ref, 1, 0), get(h_ref, 2, 0)
-    put(e_ref, 0, 0, new_ex(0, drive, hy, hz))
-    w_z = plus(plus(unpack(0, 0, monitor - 1), unpack(0, 1, monitor)), unpack(0, 2, monitor + 1))
-    w_y = plus(unpack(0, 3, monitor - 1), unpack(0, 4, monitor))
+    between_sides(drive_one)
+    ahead_e1.wait_recv()
+    hz = whole_hz(one, unpack(0, 0))
+    hy = whole_hy(one, unpack(0, 1))
+    hx, hy_prev, hz_prev = get(h_ref, 0, end), get(h_ref, 1, end - 1), get(h_ref, 2, end - 1)
+    ex = new_ex(end, drive_one, hy, hz)
+    pack(3, 1, part_z(ex, new_ey(end, get(e_ref, 1, end), hx, hz, hz_prev), hz))
+    pack(3, 0, part_y(ex, new_ez(end, hx, hy, hy_prev), hy))
+    ahead_w2.start()
+
+    first_x(drive_one)
+    first_yz_ahead(one, two, 1, ahead_e2)
+
+    h_plane(0)
+    h_plane(1)
+
+    def both(x, held):
+        e_middle(x, drive)
+        h_plane(x + 1)
+        return held
+
+    lax.fori_loop(1, end - 2, both, 0)
+    e_middle(end - 2, drive)
+    end_fields(one, drive_one)
+    copy_w(two, 1).wait_send()
+    copy_w(two, 0).wait_send()
+    partial_z(two)
+    copy_w(two, 1).start()
+    partial_y(two)
+    h_plane(end - 1)
+    hx_plane(end)
+
+    ahead_e2.wait_recv()
+    hz = whole_hz(two, unpack(1, 0))
+    hy = whole_hy(two, unpack(1, 1))
+    ex = new_ex(end, drive, hy, hz)
+    ey = new_ey(end, get(e_ref, 1, end), get(h_ref, 0, end), hz, get(h_ref, 2, end - 1))
+    w_z = part_z(ex, ey, hz)
+    pack(4, 0, w_z)
+    pack(4, 1, w_z)
+    ahead_w3.start()
+
+    first_x(drive)
+    ahead_w2.wait_recv()
     ey, ez = get(e_ref, 1, 0), get(e_ref, 2, 0)
-    hy_prev, hz_prev = beside(
-        rotate(w_y, start_cos, start_sin), rotate(w_z, start_cos, start_sin), ey, ez
-    )
-    ey = new_ey(0, ey, hx, hz, hz_prev)
-    ez = new_ez(0, hx, hy, hy_prev)
+    hy_prev, hz_prev = hy_below(unpack(3, 0), ez), hz_below(unpack(3, 1), ey)
+    ey = new_ey(0, ey, get(h_ref, 0, 0), get(h_ref, 2, 0), hz_prev)
+    ez = new_ez(0, get(h_ref, 0, 0), get(h_ref, 1, 0), hy_prev)
     put_plane(ahead_ref, 0, 0, ey)
     put_plane(ahead_ref, 0, 1, ez)
-    pack(2, [(ey, monitor), (ez, monitor), (ez, monitor - 1)])
-    late_e.start()
-
-    copy_e(slot).wait_recv()
-    complete_h(slot)
-    e_middle(end, drive)
-    copy_w(later).wait_send()
-    partial_h(later)
-    pack(1, [(get_plane(out_w, later, 1), monitor)])
-    late_w.start()
-    copy_w(later).start()
+    pack(2, 0, ey)
+    pack(2, 1, ez)
+    ahead_e3.start()
+    copy_w(two, 0).start()
+    e_middle(end - 1, drive)
 
     h_plane(1)
     h_plane(2)
 
-    def both(x, total):
+    def both_power(x, total):
         e_middle(x, last_drive)
         h_plane(x + 1)
         return power(x, total)
 
-    total = lax.fori_loop(2, end - 1, both, empty)
+    total = lax.fori_loop(2, end - 2, both_power, empty)
+    e_middle(end - 2, last_drive)
+    total = power(end - 2, total)
+
+    end_fields(two, drive)
+    give_w(three)
+    h_plane(end - 1)
+    hx_plane(end)
     e_middle(end - 1, last_drive)
     total = power(end - 1, total)
-    hx_plane(end)
-
-    def first_plane():
-        copy_w(slot).wait_recv()
-        hx, hy, hz = get(h_ref, 0, 0), get(h_ref, 1, 0), get(h_ref, 2, 0)
-        hy_prev, hz_prev = got_beside(slot)
-        ey = new_ey(0, get(e_ref, 1, 0), hx, hz, hz_prev)
-        ez = new_ez(0, hx, hy, hy_prev)
-        put(e_ref, 1, 0, ey)
-        put(e_ref, 2, 0, ez)
-        copy_e(later).wait_send()
-        put_plane(out_e, later, 0, ey)
-        put_plane(out_e, later, 1, ez)
-        copy_e(later).start()
-
-    first_plane()
+
     ex, ey, ez = get(e_ref, 0, 0), get_plane(ahead_ref, 0, 0), get_plane(ahead_ref, 0, 1)
     hx = new_hx(0, ey, ez)
     hy = new_hy(0, ex, ez, get(e_ref, 2, 1))
     hz = new_hz(0, ex, ey, get(e_ref, 1, 1))
     hx1, hy1, hz1 = get(h_ref, 0, 1), get(h_ref, 1, 1), get(h_ref, 2, 1)
-    late_w.wait_recv()
-    hz_prev = rotate(unpack(1, 0, monitor), start_cos, start_sin)
-    hz_prev = tuple(w + h_gain * e for w, e in zip(hz_prev, ey))
+    ahead_w3.wait_recv()
+    hz_prev = hz_below(unpack(4, 1), ey)
     for value in (
         new_ex(0, last_drive, hy, hz)
         + new_ey(0, ey, hx, hz, hz_prev)
@@ -584,14 +684,10 @@
         + new_ey(1, get(e_ref, 1, 1), hx1, hz1, hz)
     ):
         total = total + value * value
-    late_e.wait_recv()
-    beyond_y = rotate(unpack(2, 0, monitor), end_cos, end_sin)
-    beyond_z = plus(unpack(2, 1, monitor), unpack(2, 2, monitor - 1))
-    beyond_z = rotate(beyond_z, end_cos, end_sin)
-    w_y, w_z = get_plane(out_w, later, 0), get_plane(out_w, later, 1)
+    ahead_e3.wait_recv()
     hx = get(h_ref, 0, end)
-    hy = tuple(w - h_gain * b for w, b in zip(w_y, beyond_z))
-    hz = tuple(w + h_gain * b for w, b in zip(w_z, beyond_y))
+    hz = whole_hz(three, unpack(2, 0))
+    hy = whole_hy(three, unpack(2, 1))
     for value in new_ex(end, last_drive, hy, hz) + new_ey(
         end, get(e_ref, 1, end), hx, hz, get(h_ref, 2, end - 1)
     ):
@@ -600,17 +696,20 @@
     lax.fori_loop(1, everyone, tell_start, 0)
     got_report[me] = report_ref[...]
 
+    first_y(two, three, True, True)
+    first_z(two, three, True, True)
+
     h_plane(0)
     e_middle(1, last_drive)
-    copy_w(later).wait_recv()
-    e_first(later, last_drive)
-    copy_e(later).wait_recv()
-    complete_h(later)
-    e_middle(end, last_drive)
+    first_x(last_drive)
+    first_y(three, two, False, False)
+    first_z(three, two, False, False)
+    end_fields(three, last_drive)
     for at in range(2):
-        copy_e(at).wait_send()
-        copy_w(at).wait_send()
-    for copy in (early_w, late_w, late_e):
+        for member in range(2):
+            copy_e(at, member).wait_send()
+            copy_w(at, member).wait_send()
+    for copy in (ahead_e1, ahead_e2, ahead_e3, ahead_w2, ahead_w3):
         copy.wait_send()
     everything = got_report.at[pl.ds(0, everyone - 1)]
     pltpu.make_async_copy(everything, everything, recv_report).wait()
@@ -685,19 +784,19 @@
             pltpu.VMEM(plane, f32),
             pltpu.VMEM(plane, f32),
             pltpu.VMEM(plane, f32),
-            pltpu.VMEM((3, 16, width), f32),
-            pltpu.VMEM((3, 16, width), f32),
+            pltpu.VMEM((5, 2, 8, 2 * width), f32),
+            pltpu.VMEM((5, 2, 8, 2 * width), f32),
             pltpu.VMEM((1, 4, width, depth), f32),
-            pltpu.SemaphoreType.DMA((2,)),
-            pltpu.SemaphoreType.DMA((2,)),
-            pltpu.SemaphoreType.DMA((2,)),
-            pltpu.SemaphoreType.DMA((2,)),
-            pltpu.SemaphoreType.DMA((3,)),
-            pltpu.SemaphoreType.DMA((3,)),
+            pltpu.SemaphoreType.DMA((2, 2)),
+            pltpu.SemaphoreType.DMA((2, 2)),
+            pltpu.SemaphoreType.DMA((2, 2)),
+            pltpu.SemaphoreType.DMA((2, 2)),
+            pltpu.SemaphoreType.DMA((5,)),
+            pltpu.SemaphoreType.DMA((5,)),
             pltpu.SemaphoreType.DMA((12,)),
             pltpu.SemaphoreType.DMA,
             pltpu.SemaphoreType.DMA,
-            pltpu.SemaphoreType.REGULAR((max(everyone.bit_length(), 1),)),
+            pltpu.SemaphoreType.REGULAR((2 + everyone.bit_length(),)),
         ],
         compiler_params=pltpu.CompilerParams(
             collective_id=0, has_side_effects=True, vmem_limit_bytes=40 * 1024 * 1024

time: 68.5 us -> 67.2 us (0.981)
  Pallas kernels: 67.1 us -> 65.7 us
    pallas_call x1, Pallas kernels: 64.3 us -> 63 us  [one_point(): pl.pallas_call(kernel, out_shape=(jax.ShapeDtypeStruct(electric.shape, f3...]
where the time goes in v3:
time: 67.2 us; the launch traced here: 67 us
  Pallas kernels  65.7 us (98%)
  between operations  1.29 us (2%)
    pallas_call x1, Pallas kernels, one_point(): pl.pallas_call(kernel, out_shape=(jax.ShapeDtypeStruct(electric.shape, f3...  63 us
    pallas_call x1, Pallas kernels, one_point(): pl.pallas_call(write_out, out_shape=(pltpu.HBM(electric.shape, f32), pltp...  2.79 us

profile of v3, /device:TPU:0, one launch (start us, length us, event | category | flops | bytes accessed | tf_op | source)
XLA Modules:
  0.0 67.0 jit_solution(5039334627540762766)
XLA Ops:
  1.3 63.0 %shard_map.111 = (f32[1,6,16,64,128]{4,3,2,1,0:T(8,128)S(1)}, f32[1,6,16,64,128]{4,3,2,1,0:T(8,128)S(1)}, f32[8,128]{1,0:T(8,128)S(1)}) custom-call(s32[1,2]{1,0:T(1,128)} %bloch_in.1, f32[3]{0:T(128)} %perm_in.1, f32[1]{0:T(128)S(6)} %copy.12.peak_in, f32[10]{0:T(128)} %wave_in.1, s32[16,64,128]{2,1,0:T(8,128)} %material_in.1, f32[1,2,16,64]{3,2,1,0:T(8,128)} %sheet_in.1, ...), custom_call_target="tpu_custom_call" | custom-call | tf_op jit(solution)/shard_map/pallas_call | solution.py:760
  64.2 2.8 %shard_map.112 = (f32[1,6,16,64,128]{4,3,2,1,0:T(8,128)}, f32[1,6,16,64,128]{4,3,2,1,0:T(8,128)}, f32[1,2]{1,0:T(1,128)}, f32[2]{0:T(128)}) custom-call(f32[1,6,16,64,128]{4,3,2,1,0:T(8,128)S(1)} %get-tuple-element.7.e_ref, f32[1,6,16,64,128]{4,3,2,1,0:T(8,128)S(1)} %get-tuple-element.8.h_ref, f32[8,128]{1,0:T(8,128)S(1)} %get-tuple-element.9.power_ref), custom_call_target="tpu_custom_call" | custom-call | tf_op jit(solution)/shard_map/pallas_call | solution.py:805

commit v4 on v3

--- a/solution.py
+++ b/solution.py
@@ -87,15 +87,82 @@
     def place(at):
         return {"ka": lax.div(at, slabs), "sp": lax.rem(at, slabs)}
 
+    barrier = pltpu.get_barrier_semaphore()
+
+    def greet(other):
+        pl.semaphore_signal(barrier, inc=1, device_id=place(other), device_id_type=MESH)
+
+    grid = groups % 4 == 0
+    ahead_of = [("flip", 1), ("flip", 2)]
+    stride = 1
+    while stride < groups // 4 - 1:
+        ahead_of.insert(0, ("line", 4 * stride))
+        stride *= 2
+    ahead_of = sorted(ahead_of[:-2], key=lambda turn: turn[1]) + ahead_of[-2:]
+    stride = 1
+    while stride < slabs // 2:
+        ahead_of.append(("ring", stride))
+        stride *= 2
+    rounds = len(ahead_of) if grid else 0
+
+    def peers(kind, stride):
+        if kind == "flip":
+            return [((group + stride * (1 - 2 * lax.rem(lax.div(group, stride), 2))) * slabs + slab, None)]
+        if kind == "ring":
+            return [
+                (group * slabs + lax.rem(slab + stride, slabs), None),
+                (group * slabs + lax.rem(slab + slabs - stride, slabs), None),
+            ]
+        return [
+            ((group + stride) * slabs + slab, group + stride < groups),
+            ((group - stride) * slabs + slab, group >= stride),
+        ]
+
+    def signal_to(semaphore, found):
+        for other, exists in found:
+
+            def signal():
+                pl.semaphore_signal(
+                    semaphore, inc=1, device_id=place(other), device_id_type=MESH
+                )
+
+            if exists is None:
+                signal()
+            else:
+                pl.when(exists)(signal)
+
+    def amount(found):
+        return sum(1 if exists is None else exists.astype(jnp.int32) for _, exists in found)
+
+    if grid:
+        nearest = peers("ring", 1) + peers("flip", 1) + peers("flip", 2) + peers("line", 4)
+        signal_to(barrier, nearest)
+        greeted = amount(nearest)
+    else:
+
+        def greet_at(offset, carry):
+            signal_to(barrier, [(lax.rem(me + offset, everyone), None)])
+            return carry
+
+        lax.fori_loop(1, everyone, greet_at, 0)
+        greeted = everyone - 1
+
+    def spread(turn):
+        signal_to(entered.at[turn], peers(*ahead_of[turn]))
+
+    def learn(turn):
+        pl.semaphore_wait(entered.at[turn], amount(peers(*ahead_of[turn])))
+
     last_row = rows - 1
     loads = [
         pltpu.make_async_copy(src, dst, load_sem.at[at])
         for at, (src, dst) in enumerate(
             (
-                (e_hbm.at[0, :, 0], e_in.at[0, :, 0]),
+                (e_hbm.at[0, pl.ds(2, 4), 0], e_in.at[0, pl.ds(2, 4), 0]),
                 (e_hbm.at[0, :, last_row], e_in.at[0, :, last_row]),
                 (h_hbm.at[0, :, last_row], h_in.at[0, :, last_row]),
                 (h_hbm.at[0, :, 0], h_in.at[0, :, 0]),
+                (e_hbm.at[0, pl.ds(0, 2), 0], e_in.at[0, pl.ds(0, 2), 0]),
                 (bloch_in, bloch_ref),
                 (perm_in, perm_ref),
                 (peak_in, peak_ref),
@@ -110,73 +177,23 @@
     for load in loads:
         load.start()
 
-    barrier = pltpu.get_barrier_semaphore()
-
-    def greet(other):
-        pl.semaphore_signal(barrier, inc=1, device_id=place(other), device_id_type=MESH)
-
-    grid = groups % 4 == 0
-    ahead_of = [("flip", 1), ("flip", 2)]
-    stride = 1
-    while stride < groups // 4 - 1:
-        ahead_of.insert(0, ("line", 4 * stride))
-        stride *= 2
-    ahead_of = sorted(ahead_of[:-2], key=lambda turn: turn[1]) + ahead_of[-2:]
-    stride = 1
-    while stride < slabs // 2:
-        ahead_of.append(("ring", stride))
-        stride *= 2
-    rounds = len(ahead_of) if grid else 0
-
-    def peers(kind, stride):
-        if kind == "flip":
-            return [((group + stride * (1 - 2 * lax.rem(lax.div(group, stride), 2))) * slabs + slab, None)]
-        if kind == "ring":
-            return [
-                (group * slabs + lax.rem(slab + stride, slabs), None),
-                (group * slabs + lax.rem(slab + slabs - stride, slabs), None),
-            ]
-        return [
-            ((group + stride) * slabs + slab, group + stride < groups),
-            ((group - stride) * slabs + slab, group >= stride),
-        ]
-
-    def signal_to(semaphore, found):
-        for other, exists in found:
-
-            def signal():
-                pl.semaphore_signal(
-                    semaphore, inc=1, device_id=place(other), device_id_type=MESH
-                )
-
-            if exists is None:
-                signal()
-            else:
-                pl.when(exists)(signal)
-
-    def amount(found):
-        return sum(1 if exists is None else exists.astype(jnp.int32) for _, exists in found)
-
-    if grid:
-        nearest = peers("ring", 1) + peers("flip", 1) + peers("flip", 2) + peers("line", 4)
-        signal_to(barrier, nearest)
-        greeted = amount(nearest)
-    else:
-
-        def greet_at(offset, carry):
-            signal_to(barrier, [(lax.rem(me + offset, everyone), None)])
-            return carry
-
-        lax.fori_loop(1, everyone, greet_at, 0)
-        greeted = everyone - 1
-
-    def spread(turn):
-        signal_to(entered.at[turn], peers(*ahead_of[turn]))
-
-    def learn(turn):
-        pl.semaphore_wait(entered.at[turn], amount(peers(*ahead_of[turn])))
-
-    for load in loads[4:8]:
+    def copy_e(slot, member):
+        return pltpu.make_async_remote_copy(
+            src_ref=out_e.at[slot, pl.ds(2 * member, 2)],
+            dst_ref=got_e.at[slot, pl.ds(2 * member, 2)],
+            send_sem=send_e.at[slot, member],
+            recv_sem=recv_e.at[slot, member],
+            device_id={"sp": lower},
+            device_id_type=MESH,
+        )
+
+    loads[0].wait()
+    for member in range(4):
+        out_e[0, member] = e_in[0, 2 + member, 0].astype(jnp.float32)
+    pl.semaphore_wait(barrier, greeted)
+    copy_e(0, 0).start()
+    copy_e(0, 1).start()
+    for load in loads[5:9]:
         load.wait()
 
     height = lax.broadcasted_iota(jnp.int32, (8, depth), 1).astype(jnp.float32)
@@ -329,18 +346,18 @@
         put(e_ref, 2, x, ez)
         return ey, ez
 
+    def e_middle_xy(x, drive):
+        hx, hy, hz = get(h_ref, 0, x), get(h_ref, 1, x), get(h_ref, 2, x)
+        put(e_ref, 0, x, new_ex(x, drive, hy, hz))
+        put(e_ref, 1, x, new_ey(x, get(e_ref, 1, x), hx, hz, get(h_ref, 2, x - 1)))
+
+    def e_middle_z(x, carry):
+        hx, hy = get(h_ref, 0, x), get(h_ref, 1, x)
+        put(e_ref, 2, x, new_ez(x, hx, hy, get(h_ref, 1, x - 1)))
+        return carry
+
     def e_middle(x, drive):
         return e_update(x, drive, get(h_ref, 1, x - 1), get(h_ref, 2, x - 1))
-
-    def copy_e(slot, member):
-        return pltpu.make_async_remote_copy(
-            src_ref=out_e.at[slot, pl.ds(2 * member, 2)],
-            dst_ref=got_e.at[slot, pl.ds(2 * member, 2)],
-            send_sem=send_e.at[slot, member],
-            recv_sem=recv_e.at[slot, member],
-            device_id={"sp": lower},
-            device_id_type=MESH,
-        )
 
     def copy_w(slot, member):
         return pltpu.make_async_remote_copy(
@@ -386,13 +403,7 @@
             h_ref[0, member, x] = h_in[0, member, x].astype(jnp.float32)
         return carry
 
-    loads[0].wait()
-    for member in range(4):
-        out_e[0, member] = e_in[0, 2 + member, 0].astype(jnp.float32)
-    pl.semaphore_wait(barrier, greeted)
-    copy_e(0, 0).start()
-    copy_e(0, 1).start()
-    for load in loads[1:4]:
+    for load in loads[1:5]:
         load.wait()
     widen(rows - 1, 0)
     partial_z(0)
@@ -400,7 +411,7 @@
     partial_y(0)
     copy_w(0, 0).start()
     widen(0, 0)
-    for load in loads[8:]:
+    for load in loads[9:]:
         load.wait()
     lax.fori_loop(1, rows - 1, widen, 0)
 
@@ -420,7 +431,14 @@
             drive_ref[part, x] = jnp.where(lane == PML + 2, column, 0.0)
         return carry
 
-    lax.fori_loop(0, rows, prepare, 0)
+    together = 4 if rows % 4 == 0 else 1
+
+    def prepare_some(group_of, carry):
+        for at in range(together):
+            prepare(group_of * together + at, carry)
+        return carry
+
+    lax.fori_loop(0, rows // together, prepare_some, 0)
 
     def power(x, total):
         for member in range(4):
@@ -428,14 +446,11 @@
             total = total + value * value
         return total
 
-    row_lane = lax.broadcasted_iota(jnp.int32, (1, depth), 1)
     empty = jnp.zeros((width, depth), jnp.float32)
     assert steps % (2 * INTERVAL) == 0 and rows > 6
 
     def note(total, at):
-        amount = jnp.sum(jnp.where(lane == monitor, total, 0.0), axis=0, keepdims=True)
-        amount = jnp.sum(amount, axis=1, keepdims=True)
-        report_ref[...] += jnp.where(row_lane == at, amount, 0.0)
+        report_ref[pl.ds(at, 1)] = jnp.sum(total, axis=0, keepdims=True)
 
     def first_y(slot, later, sent, go):
         copy_w(slot, 1).wait_recv()
@@ -655,19 +670,19 @@
     h_plane(2)
 
     def both_power(x, total):
-        e_middle(x, last_drive)
+        e_middle_xy(x, last_drive)
         h_plane(x + 1)
         return power(x, total)
 
     total = lax.fori_loop(2, end - 2, both_power, empty)
-    e_middle(end - 2, last_drive)
+    e_middle_xy(end - 2, last_drive)
     total = power(end - 2, total)
 
     end_fields(two, drive)
     give_w(three)
     h_plane(end - 1)
     hx_plane(end)
-    e_middle(end - 1, last_drive)
+    e_middle_xy(end - 1, last_drive)
     total = power(end - 1, total)
 
     ex, ey, ez = get(e_ref, 0, 0), get_plane(ahead_ref, 0, 0), get_plane(ahead_ref, 0, 1)
@@ -699,6 +714,7 @@
     first_y(two, three, True, True)
     first_z(two, three, True, True)
 
+    lax.fori_loop(2, end, e_middle_z, 0)
     h_plane(0)
     e_middle(1, last_drive)
     first_x(last_drive)
@@ -718,11 +734,11 @@
     def gather(at, held):
         return held + got_report[group * slabs + at]
 
-    ours = lax.fori_loop(0, slabs, gather, jnp.zeros((1, depth), jnp.float32))
+    ours = lax.fori_loop(0, slabs, gather, jnp.zeros(report_ref.shape, jnp.float32))
     total = jnp.sum(got_report[...], axis=0)
     cells = rows * slabs * width
-    power_ref[0:1] = ours / cells
-    power_ref[1:2] = total / cells / groups
+    power_ref[0] = ours / cells
+    power_ref[1] = total / cells / groups
 
 
 def write_out(e_ref, h_ref, power_ref, e_out, h_out, reflected_out, mean_out, own, mean, sems):
@@ -735,10 +751,11 @@
     ]
     for write in writes:
         write.start()
-    lane = lax.broadcasted_iota(jnp.int32, (1, power_ref.shape[1]), 1)
+    lane = lax.broadcasted_iota(jnp.int32, (1, power_ref.shape[2]), 1)
+    chosen = lane == PML + 6
     for at in range(snaps):
-        own[0, at] = jnp.sum(jnp.where(lane == at, power_ref[0:1], 0.0))
-        mean[at] = jnp.sum(jnp.where(lane == at, power_ref[1:2], 0.0))
+        own[0, at] = jnp.sum(jnp.where(chosen, power_ref[0, at : at + 1], 0.0))
+        mean[at] = jnp.sum(jnp.where(chosen, power_ref[1, at : at + 1], 0.0))
     small = [
         pltpu.make_async_copy(own, reflected_out, sems.at[0, members]),
         pltpu.make_async_copy(mean, mean_out, sems.at[1, members]),
@@ -762,7 +779,7 @@
         out_shape=(
             jax.ShapeDtypeStruct(electric.shape, f32),
             jax.ShapeDtypeStruct(magnetic.shape, f32),
-            jax.ShapeDtypeStruct((8, depth), f32),
+            jax.ShapeDtypeStruct((2, snaps, depth), f32),
         ),
         in_specs=[hbm] * 8,
         out_specs=(vmem, vmem, vmem),
@@ -775,8 +792,8 @@
             pltpu.VMEM(sheet.shape, f32),
             pltpu.VMEM(electric.shape, electric.dtype),
             pltpu.VMEM(magnetic.shape, magnetic.dtype),
-            pltpu.VMEM((1, depth), f32),
-            pltpu.VMEM((everyone, 1, depth), f32),
+            pltpu.VMEM((snaps, depth), f32),
+            pltpu.VMEM((everyone, snaps, depth), f32),
             pltpu.VMEM((rows, width, depth), f32),
             pltpu.VMEM((rows, width, depth), f32),
             pltpu.VMEM((2, rows, width, depth), f32),
@@ -793,7 +810,7 @@
             pltpu.SemaphoreType.DMA((2, 2)),
             pltpu.SemaphoreType.DMA((5,)),
             pltpu.SemaphoreType.DMA((5,)),
-            pltpu.SemaphoreType.DMA((12,)),
+            pltpu.SemaphoreType.DMA((13,)),
             pltpu.SemaphoreType.DMA,
             pltpu.SemaphoreType.DMA,
             pltpu.SemaphoreType.REGULAR((2 + everyone.bit_length(),)),

time: 67.2 us -> 67.3 us (level)
  no operation moved by 1% of the time
where the time goes in v4:
time: 67.3 us; the launch traced here: 67.1 us
  Pallas kernels  65.8 us (98%)
  between operations  1.29 us (2%)
    pallas_call x1, Pallas kernels, one_point(): pl.pallas_call(kernel, out_shape=(jax.ShapeDtypeStruct(electric.shape, f3...  63.1 us
    pallas_call x1, Pallas kernels, one_point(): pl.pallas_call(write_out, out_shape=(pltpu.HBM(electric.shape, f32), pltp...  2.79 us

profile of v4, /device:TPU:0, one launch (start us, length us, event | category | flops | bytes accessed | tf_op | source)
XLA Modules:
  0.0 67.1 jit_solution(17508858652097067554)
XLA Ops:
  1.3 63.1 %shard_map.111 = (f32[1,6,16,64,128]{4,3,2,1,0:T(8,128)S(1)}, f32[1,6,16,64,128]{4,3,2,1,0:T(8,128)S(1)}, f32[2,2,128]{2,1,0:T(2,128)S(1)}) custom-call(s32[1,2]{1,0:T(1,128)} %bloch_in.1, f32[3]{0:T(128)} %perm_in.1, f32[1]{0:T(128)S(6)} %copy.12.peak_in, f32[10]{0:T(128)} %wave_in.1, s32[16,64,128]{2,1,0:T(8,128)} %material_in.1, ...), custom_call_target="tpu_custom_call" | custom-call | tf_op jit(solution)/shard_map/pallas_call | solution.py:777
  64.3 2.8 %shard_map.112 = (f32[1,6,16,64,128]{4,3,2,1,0:T(8,128)}, f32[1,6,16,64,128]{4,3,2,1,0:T(8,128)}, f32[1,2]{1,0:T(1,128)}, f32[2]{0:T(128)}) custom-call(f32[1,6,16,64,128]{4,3,2,1,0:T(8,128)S(1)} %get-tuple-element.7.e_ref, f32[1,6,16,64,128]{4,3,2,1,0:T(8,128)S(1)} %get-tuple-element.8.h_ref, f32[2,2,128]{2,1,0:T(2,128)S(1)} %get-tuple-element.9.power_ref), custom_call_target="tpu_custom_call" | custom-call | tf_op jit(solution)/shard_map/pallas_call | solution.py:822

commit v5 on v4

--- a/solution.py
+++ b/solution.py
@@ -346,16 +346,6 @@
         put(e_ref, 2, x, ez)
         return ey, ez
 
-    def e_middle_xy(x, drive):
-        hx, hy, hz = get(h_ref, 0, x), get(h_ref, 1, x), get(h_ref, 2, x)
-        put(e_ref, 0, x, new_ex(x, drive, hy, hz))
-        put(e_ref, 1, x, new_ey(x, get(e_ref, 1, x), hx, hz, get(h_ref, 2, x - 1)))
-
-    def e_middle_z(x, carry):
-        hx, hy = get(h_ref, 0, x), get(h_ref, 1, x)
-        put(e_ref, 2, x, new_ez(x, hx, hy, get(h_ref, 1, x - 1)))
-        return carry
-
     def e_middle(x, drive):
         return e_update(x, drive, get(h_ref, 1, x - 1), get(h_ref, 2, x - 1))
 
@@ -446,11 +436,14 @@
             total = total + value * value
         return total
 
+    row_lane = lax.broadcasted_iota(jnp.int32, (1, depth), 1)
     empty = jnp.zeros((width, depth), jnp.float32)
     assert steps % (2 * INTERVAL) == 0 and rows > 6
 
     def note(total, at):
-        report_ref[pl.ds(at, 1)] = jnp.sum(total, axis=0, keepdims=True)
+        amount = jnp.sum(jnp.where(lane == monitor, total, 0.0), axis=0, keepdims=True)
+        amount = jnp.sum(amount, axis=1, keepdims=True)
+        report_ref[...] += jnp.where(row_lane == at, amount, 0.0)
 
     def first_y(slot, later, sent, go):
         copy_w(slot, 1).wait_recv()
@@ -670,19 +663,19 @@
     h_plane(2)
 
     def both_power(x, total):
-        e_middle_xy(x, last_drive)
+        e_middle(x, last_drive)
         h_plane(x + 1)
         return power(x, total)
 
     total = lax.fori_loop(2, end - 2, both_power, empty)
-    e_middle_xy(end - 2, last_drive)
+    e_middle(end - 2, last_drive)
     total = power(end - 2, total)
 
     end_fields(two, drive)
     give_w(three)
     h_plane(end - 1)
     hx_plane(end)
-    e_middle_xy(end - 1, last_drive)
+    e_middle(end - 1, last_drive)
     total = power(end - 1, total)
 
     ex, ey, ez = get(e_ref, 0, 0), get_plane(ahead_ref, 0, 0), get_plane(ahead_ref, 0, 1)
@@ -714,7 +707,6 @@
     first_y(two, three, True, True)
     first_z(two, three, True, True)
 
-    lax.fori_loop(2, end, e_middle_z, 0)
     h_plane(0)
     e_middle(1, last_drive)
     first_x(last_drive)
@@ -734,11 +726,11 @@
     def gather(at, held):
         return held + got_report[group * slabs + at]
 
-    ours = lax.fori_loop(0, slabs, gather, jnp.zeros(report_ref.shape, jnp.float32))
+    ours = lax.fori_loop(0, slabs, gather, jnp.zeros((1, depth), jnp.float32))
     total = jnp.sum(got_report[...], axis=0)
     cells = rows * slabs * width
-    power_ref[0] = ours / cells
-    power_ref[1] = total / cells / groups
+    power_ref[0:1] = ours / cells
+    power_ref[1:2] = total / cells / groups
 
 
 def write_out(e_ref, h_ref, power_ref, e_out, h_out, reflected_out, mean_out, own, mean, sems):
@@ -751,11 +743,10 @@
     ]
     for write in writes:
         write.start()
-    lane = lax.broadcasted_iota(jnp.int32, (1, power_ref.shape[2]), 1)
-    chosen = lane == PML + 6
+    lane = lax.broadcasted_iota(jnp.int32, (1, power_ref.shape[1]), 1)
     for at in range(snaps):
-        own[0, at] = jnp.sum(jnp.where(chosen, power_ref[0, at : at + 1], 0.0))
-        mean[at] = jnp.sum(jnp.where(chosen, power_ref[1, at : at + 1], 0.0))
+        own[0, at] = jnp.sum(jnp.where(lane == at, power_ref[0:1], 0.0))
+        mean[at] = jnp.sum(jnp.where(lane == at, power_ref[1:2], 0.0))
     small = [
         pltpu.make_async_copy(own, reflected_out, sems.at[0, members]),
         pltpu.make_async_copy(mean, mean_out, sems.at[1, members]),
@@ -779,7 +770,7 @@
         out_shape=(
             jax.ShapeDtypeStruct(electric.shape, f32),
             jax.ShapeDtypeStruct(magnetic.shape, f32),
-            jax.ShapeDtypeStruct((2, snaps, depth), f32),
+            jax.ShapeDtypeStruct((8, depth), f32),
         ),
         in_specs=[hbm] * 8,
         out_specs=(vmem, vmem, vmem),
@@ -792,8 +783,8 @@
             pltpu.VMEM(sheet.shape, f32),
             pltpu.VMEM(electric.shape, electric.dtype),
             pltpu.VMEM(magnetic.shape, magnetic.dtype),
-            pltpu.VMEM((snaps, depth), f32),
-            pltpu.VMEM((everyone, snaps, depth), f32),
+            pltpu.VMEM((1, depth), f32),
+            pltpu.VMEM((everyone, 1, depth), f32),
             pltpu.VMEM((rows, width, depth), f32),
             pltpu.VMEM((rows, width, depth), f32),
             pltpu.VMEM((2, rows, width, depth), f32),

time: 67.3 us -> 67.2 us (level)
  no operation moved by 1% of the time
where the time goes in v5:
time: 67.2 us; the launch traced here: 67 us
  Pallas kernels  65.7 us (98%)
  between operations  1.29 us (2%)
    pallas_call x1, Pallas kernels, one_point(): pl.pallas_call(kernel, out_shape=(jax.ShapeDtypeStruct(electric.shape, f3...  62.9 us
    pallas_call x1, Pallas kernels, one_point(): pl.pallas_call(write_out, out_shape=(pltpu.HBM(electric.shape, f32), pltp...  2.79 us

profile of v5, /device:TPU:0, one launch (start us, length us, event | category | flops | bytes accessed | tf_op | source)
XLA Modules:
  0.0 67.0 jit_solution(11985751627624821821)
XLA Ops:
  1.3 62.9 %shard_map.111 = (f32[1,6,16,64,128]{4,3,2,1,0:T(8,128)S(1)}, f32[1,6,16,64,128]{4,3,2,1,0:T(8,128)S(1)}, f32[8,128]{1,0:T(8,128)S(1)}) custom-call(s32[1,2]{1,0:T(1,128)} %bloch_in.1, f32[3]{0:T(128)} %perm_in.1, f32[1]{0:T(128)S(6)} %copy.12.peak_in, f32[10]{0:T(128)} %wave_in.1, s32[16,64,128]{2,1,0:T(8,128)} %material_in.1, f32[1,2,16,64]{3,2,1,0:T(8,128)} %sheet_in.1, ...), custom_call_target="tpu_custom_call" | custom-call | tf_op jit(solution)/shard_map/pallas_call | solution.py:768
  64.2 2.8 %shard_map.112 = (f32[1,6,16,64,128]{4,3,2,1,0:T(8,128)}, f32[1,6,16,64,128]{4,3,2,1,0:T(8,128)}, f32[1,2]{1,0:T(1,128)}, f32[2]{0:T(128)}) custom-call(f32[1,6,16,64,128]{4,3,2,1,0:T(8,128)S(1)} %get-tuple-element.7.e_ref, f32[1,6,16,64,128]{4,3,2,1,0:T(8,128)S(1)} %get-tuple-element.8.h_ref, f32[8,128]{1,0:T(8,128)S(1)} %get-tuple-element.9.power_ref), custom_call_target="tpu_custom_call" | custom-call | tf_op jit(solution)/shard_map/pallas_call | solution.py:813
